TPU v7x, 32 devices: a whole 2x2x4 slice. The times are simulated.
32 devices in a mesh: gx: 4 (over z), gy: 2 (over x), gz: 4 (over y, core).
Axes of the slice: x: 2, y: 2, z: 4, core: 2. Of those that a mesh axis runs over, the one named last changes fastest.
Arguments:
- old_slots: bfloat16 [4, 2, 32, 4096], P('gx', 'gy', 'gz'), may hold values from -6 to 6
- old_ids: int32 [4, 2, 32], P('gx', 'gy', 'gz'), may hold values from -1 to 31, as said below
- old_owner: int32 [4, 2, 32], P('gx', 'gy'), may hold values from 0 to 3, as said below
- coefficient: float32 [64, 32, 512], P('gx', 'gy', 'gz'), may hold values from 0.2 to 5
Outputs:
- solution: float32 [64, 32, 512], P('gx', 'gy', 'gz')
Inputs may be any that keep to these rules, and one draw needn't show every extreme that they name: old_owner[a, c, b] is the index along gz of the device that held box b of box column (a, c) before the move; no device holds more than 8 boxes of a column and some device holds exactly 8; no device holds more than 2 of the 8 boxes with one value of b // 8, and that bound is reached. old_ids[a, c, g * 8 + q] is the box held in slot q of device g of box column (a, c), or -1 for an empty slot; it agrees with old_owner and each box stands in exactly one slot.
All inputs are finite; a program needn't handle non-finite values.
Results may differ from a plain program's by a relative error of at most 0.0003.
Values may be sent and summed in bfloat16 or wider, within the bound.
A program may use at most 64 MiB of HBM per device.

v0:
```python
import jax
import jax.numpy as jnp
from jax import lax
from jax.sharding import PartitionSpec as P

BOX = 16
NB = 8
SEND = 2
SWEEPS = 2


def with_halo(cells, sides, width):
    for axis, dim in sides:
        count = lax.axis_size(axis)
        ends = count - 1
        head = lax.slice_in_dim(cells, 0, width, axis=dim)
        tail = lax.slice_in_dim(cells, cells.shape[dim] - width, cells.shape[dim], axis=dim)
        cells = jnp.concatenate(
            [
                lax.ppermute(tail, axis, [(i, (i + 1) % count) for i in range(ends)]),
                cells,
                lax.ppermute(head, axis, [((i + 1) % count, i) for i in range(ends)]),
            ],
            axis=dim,
        )
    return cells


def rims(values, depth):
    return with_halo(values, (("gx", 0), ("gy", 1), ("gz", 2)), depth)


def inner(padded):
    return padded[1:-1, 1:-1, 1:-1]


def operator_parts(padded):
    face_first = 0.5 * (padded[:-1, 1:-1, 1:-1] + padded[1:, 1:-1, 1:-1])
    face_second = 0.5 * (padded[1:-1, :-1, 1:-1] + padded[1:-1, 1:, 1:-1])
    face_third = 0.5 * (padded[1:-1, 1:-1, :-1] + padded[1:-1, 1:-1, 1:])
    diagonal = (
        face_first[:-1]
        + face_first[1:]
        + face_second[:, :-1]
        + face_second[:, 1:]
        + face_third[:, :, :-1]
        + face_third[:, :, 1:]
    )
    return (face_first, face_second, face_third, diagonal)


def neighbours(padded, stencil):
    face_first, face_second, face_third, diagonal = stencil
    summed = face_first[:-1] * padded[:-2, 1:-1, 1:-1] + face_first[1:] * padded[2:, 1:-1, 1:-1]
    summed = (
        summed
        + face_second[:, :-1] * padded[1:-1, :-2, 1:-1]
        + face_second[:, 1:] * padded[1:-1, 2:, 1:-1]
    )
    summed = (
        summed
        + face_third[:, :, :-1] * padded[1:-1, 1:-1, :-2]
        + face_third[:, :, 1:] * padded[1:-1, 1:-1, 2:]
    )
    return summed


def red_cells(shape, margin):
    index_first = lax.broadcasted_iota(jnp.int32, shape, 0)
    index_second = lax.broadcasted_iota(jnp.int32, shape, 1)
    index_third = lax.broadcasted_iota(jnp.int32, shape, 2)
    return (index_first + index_second + index_third + margin) % 2 == 0


def relax(padded, source, stencil, factor, chosen):
    fresh = (factor * source + neighbours(padded, stencil)) / stencil[3]
    return jnp.where(chosen, fresh, inner(padded))


def apply_operator(values, stencil, factor):
    return (stencil[3] * values - neighbours(rims(values, 1), stencil)) / factor


def sweep_thin(values, source, stencil, factor, red_mask, starting):
    if starting:
        values = jnp.where(red_mask, factor * source / stencil[3], 0.0)
    else:
        values = relax(rims(values, 1), source, stencil, factor, red_mask)
    return relax(rims(values, 1), source, stencil, factor, jnp.logical_not(red_mask))


def smooth_thin(values, source, stencil, factor, starting):
    red_mask = red_cells(source.shape, 0)
    for counter in range(SWEEPS):
        values = sweep_thin(values, source, stencil, factor, red_mask, starting and counter == 0)
    return values


def sweep_deep(
    values, source_rim, stencil_rim, stencil_block, factor, red_rim, black_block, starting
):
    if starting:
        coloured = jnp.where(red_rim, factor * source_rim / stencil_rim[3], 0.0)
    else:
        coloured = relax(rims(values, 2), source_rim, stencil_rim, factor, red_rim)
    return relax(coloured, inner(source_rim), stencil_block, factor, black_block)


def coarsen(values):
    extent_first, extent_second, extent_third = values.shape
    grouped = values.reshape(extent_first // 2, 2, extent_second // 2, 2, extent_third // 2, 2)
    return grouped.mean(axis=(1, 3, 5))


def refine(values):
    return jnp.repeat(jnp.repeat(jnp.repeat(values, 2, axis=0), 2, axis=1), 2, axis=2)


def dot_pair(first_term, second_term):
    return lax.psum((first_term, second_term), ("gx", "gy", "gz"))


def bottom_solve(rhs_low, stencil, factor):
    image_low = apply_operator(rhs_low, stencil, factor)
    norm_rhs, along_rhs = dot_pair(jnp.sum(rhs_low * rhs_low), jnp.sum(rhs_low * image_low))
    alpha_step = norm_rhs / along_rhs
    rest_low = rhs_low - alpha_step * image_low
    turned = apply_operator(rest_low, stencil, factor)
    turned_rest, turned_norm = dot_pair(jnp.sum(turned * rest_low), jnp.sum(turned * turned))
    omega_step = turned_rest / turned_norm
    return alpha_step * rhs_low + omega_step * rest_low


def move_boxes(old_slots, old_ids, old_owner):
    slot_rows = old_slots.reshape(old_slots.shape[2], old_slots.shape[3])
    slot_ids = old_ids.reshape(-1)
    owner_map = old_owner.reshape(-1)
    groups = lax.axis_size("gz")
    my_index = lax.axis_index("gz")
    capacity = slot_ids.shape[0]
    filled = slot_ids >= 0
    target = jnp.where(filled, slot_ids // NB, -1)
    earlier = (
        (target[None, :] == target[:, None])
        & (slot_ids[None, :] < slot_ids[:, None])
        & filled[None, :]
    )
    ranking = jnp.sum(earlier.astype(jnp.int32), axis=1)
    send_row = jnp.where(filled, target * SEND + ranking, -1)
    picker = lax.broadcasted_iota(jnp.int32, (groups * SEND, capacity), 0) == send_row[None, :]
    outgoing = jnp.dot(
        picker.astype(jnp.bfloat16), slot_rows, preferred_element_type=jnp.float32
    ).astype(jnp.bfloat16)
    incoming = lax.all_to_all(outgoing, "gz", split_axis=0, concat_axis=0, tiled=True).astype(
        jnp.float32
    )
    arriving = lax.dynamic_slice_in_dim(owner_map, my_index * NB, NB)
    later_index = lax.broadcasted_iota(jnp.int32, (NB, NB), 0)
    before = (arriving[None, :] == arriving[:, None]) & (
        lax.broadcasted_iota(jnp.int32, (NB, NB), 1) < later_index
    )
    order_within = jnp.sum(before.astype(jnp.int32), axis=1)
    chosen_boxes = jnp.take(incoming, arriving * SEND + order_within, axis=0)
    stacked = chosen_boxes.reshape(NB, BOX, BOX, BOX).transpose(1, 2, 0, 3)
    return stacked.reshape(BOX, BOX, NB * BOX)


def per_device(old_slots, old_ids, old_owner, coefficient):
    source_fine = move_boxes(old_slots, old_ids, old_owner)
    coefficient_rim = rims(coefficient, 2)
    inside = inner(coefficient_rim) > 0.0
    face_first, face_second, face_third, diagonal = operator_parts(coefficient_rim)
    stencil_rim = (face_first, face_second, face_third, jnp.where(inside, diagonal, 1.0))
    stencil_fine = (inner(face_first), inner(face_second), inner(face_third), inner(diagonal))
    source_rim = rims(source_fine, 1)
    red_rim = jnp.logical_and(red_cells(inside.shape, 1), inside)
    black_fine = jnp.logical_not(red_cells(source_fine.shape, 0))

    def smooth_fine(values, starting):
        for counter in range(SWEEPS):
            values = sweep_deep(
                values,
                source_rim,
                stencil_rim,
                stencil_fine,
                1.0,
                red_rim,
                black_fine,
                starting and counter == 0,
            )
        return values

    fine_values = smooth_fine(jnp.zeros_like(source_fine), True)
    residual_fine = source_fine - apply_operator(fine_values, stencil_fine, 1.0)
    coefficient_mid = coarsen(coefficient)
    stencil_mid = operator_parts(rims(coefficient_mid, 1))
    source_mid = coarsen(residual_fine)
    middle_values = smooth_thin(jnp.zeros_like(source_mid), source_mid, stencil_mid, 4.0, True)
    residual_mid = source_mid - apply_operator(middle_values, stencil_mid, 4.0)
    coefficient_low = coarsen(coefficient_mid)
    stencil_low = operator_parts(rims(coefficient_low, 1))
    bottom_values = bottom_solve(coarsen(residual_mid), stencil_low, 16.0)
    middle_values = smooth_thin(
        middle_values + refine(bottom_values), source_mid, stencil_mid, 4.0, False
    )
    return smooth_fine(fine_values + refine(middle_values), False)


def solution(mesh):
    in_specs = (
        P("gx", "gy", "gz", None),
        P("gx", "gy", "gz"),
        P("gx", "gy", None),
        P("gx", "gy", "gz"),
    )
    out_specs = P("gx", "gy", "gz")
    return jax.shard_map(
        per_device, mesh=mesh, in_specs=in_specs, out_specs=out_specs, check_vma=False
    )
```

profile of v0, /device:TPU:1, one launch (start us, length us, event | category | flops | bytes accessed | tf_op | source)
XLA Modules:
  0.0 550.7 jit_solution(12764030653669933789)
XLA Ops:
  2.1 4.6 collective-permute-start
  10.5 4.2 all-to-all-start
  14.7 10.6 %reshape.184 = f32[8,2,8,2,64,2]{5,4,3,2,1,0:T(8,128)} reshape(f32[16,16,128]{2,1,0:T(8,128)} %param.7) | data formatting | bytes 262144 | tf_op jit(solution)/shard_map/reshape | solution.py:111
  25.3 4.0 reduce_sum.96
  29.9 4.2 collective-permute-start.24
  43.7 5.3 collective-permute-start.4
  52.1 4.4 collective-permute-done.5
  58.6 4.3 collective-permute-start.6
  73.9 4.6 collective-permute-start.10
  81.4 4.4 collective-permute-done.11
  94.6 4.0 collective-permute-start.14
  103.3 4.0 collective-permute-start.16
  110.4 4.4 collective-permute-done.17
  117.0 4.3 collective-permute-start.18
  133.0 4.7 collective-permute-start.22
  140.5 4.4 collective-permute-done.23
  145.4 9.8 %reshape.183 = f32[8,2,8,2,64,2]{5,4,3,2,1,0:T(8,128)} reshape(f32[16,16,128]{2,1,0:T(8,128)S(1)} %fusion.55) | data formatting | bytes 262144 | tf_op jit(solution)/shard_map/reshape | solution.py:111
  155.2 4.0 reduce_sum.95
  159.4 4.3 collective-permute-start.30
  173.9 4.6 collective-permute-start.34
  180.4 3.8 collective-permute-done.35
  196.8 4.7 collective-permute-start.40
  203.5 3.8 collective-permute-done.41
  219.3 4.7 collective-permute-start.46
  237.6 3.7 collective-permute-start.50
  245.8 6.5 %collective-permute-start.52 = (f32[10,10,1]{2,1,0:T(8,128)S(1)}, f32[10,10,1]{2,1,0:T(8,128)S(1)}, u32[]{:S(2)}, u32[]{:S(2)}) collective-permute-start(f32[10,10,1]{2,1,0:T(8,128)S(1)} %get-tuple-element.61), channel_id=1, source_target_pairs={{0,1},{1,2},{2,3},{4,5},{5,6},{6,7},{8,9},{9,10},{10,11},{12,13},{... | collective-permute-start | bytes 1208 | tf_op jit(solution)/shard_map/ppermute | solution.py:20
  254.2 3.8 collective-permute-done.53
  259.4 4.3 collective-permute-start.60
  275.2 4.8 collective-permute-start.64
  285.9 37.9 %all-reduce.1 = (f32[]{:T(128)}, f32[]{:T(128)}) all-reduce(f32[]{:T(128)} %get-tuple-element.8, f32[]{:T(128)} %get-tuple-element.7), channel_id=1, replica_groups=mesh['gx'=4,'gy'=2,'gz'=4] {'gx','gy','gz'}, use_global_device_ids=true, to_apply=%region_6.7 | all-reduce | flops 2 | bytes 16 | tf_op jit(solution)/shard_map/psum | solution.py:120
  331.1 4.3 collective-permute-start.68
  339.9 7.3 %collective-permute-start.70 = (f32[6,6,1]{2,1,0:T(8,128)S(1)}, f32[6,6,1]{2,1,0:T(8,128)S(1)}, u32[]{:S(2)}, u32[]{:S(2)}) collective-permute-start(f32[6,6,1]{2,1,0:T(8,128)S(1)} %get-tuple-element.107), channel_id=1, source_target_pairs={{0,1},{1,2},{2,3},{4,5},{5,6},{6,7},{8,9},{9,10},{10,11},{12,13},{... | collective-permute-start | bytes 440 | tf_op jit(solution)/shard_map/ppermute | solution.py:20
  353.2 36.6 %all-reduce = (f32[]{:T(128)}, f32[]{:T(128)}) all-reduce(f32[]{:T(128)} %get-tuple-element.6, f32[]{:T(128)} %get-tuple-element.5), channel_id=1, replica_groups=mesh['gx'=4,'gy'=2,'gz'=4] {'gx','gy','gz'}, use_global_device_ids=true, to_apply=%region_11.12 | all-reduce | flops 2 | bytes 16 | tf_op jit(solution)/shard_map/psum | solution.py:120
  398.2 4.3 collective-permute-start.74
  407.0 7.3 %collective-permute-start.76 = (f32[10,10,1]{2,1,0:T(8,128)S(1)}, f32[10,10,1]{2,1,0:T(8,128)S(1)}, u32[]{:S(2)}, u32[]{:S(2)}) collective-permute-start(f32[10,10,1]{2,1,0:T(8,128)S(1)} %get-tuple-element.59), channel_id=1, source_target_pairs={{0,1},{1,2},{2,3},{4,5},{5,6},{6,7},{8,9},{9,10},{10,11},{12,13},{... | collective-permute-start | bytes 1208 | tf_op jit(solution)/shard_map/ppermute | solution.py:20
  416.3 3.8 collective-permute-done.77
  423.9 3.3 collective-permute-done.79
  433.1 4.4 collective-permute-start.82
  439.5 3.8 collective-permute-done.83
  443.4 3.6 collective-permute-start.84
  457.3 4.7 collective-permute-start.88
  464.0 3.8 collective-permute-done.89
  479.8 4.7 collective-permute-start.94
  486.7 3.6 collective-permute-done.95
  507.0 4.7 collective-permute-start.100
  514.8 4.4 collective-permute-done.101
  534.7 4.6 collective-permute-start.106
  542.4 4.4 collective-permute-done.107
  (362 shorter events, 254.7 us)
Async XLA Ops:
  0.8 35.1 %collective-permute-start.1 = (f32[2,16,128]{2,1,0:T(8,128)S(1)}, f32[2,16,128]{2,1,0:T(8,128)S(1)}, u32[]{:S(2)}, u32[]{:S(2)}) collective-permute-start(f32[2,16,128]{2,1,0:T(8,128)S(1)} %get-tuple-element.51), channel_id=1, source_target_pairs={{8,0},{16,8},{24,16},{9,1},{17,9},{25,17},{10,2},{18,10},{26,18},{... | collective-permute-start | bytes 49160 | tf_op jit(solution)/shard_map/ppermute | solution.py:22
  2.1 33.7 %collective-permute-start = (f32[2,16,128]{2,1,0:T(8,128)S(1)}, f32[2,16,128]{2,1,0:T(8,128)S(1)}, u32[]{:S(2)}, u32[]{:S(2)}) collective-permute-start(f32[2,16,128]{2,1,0:T(8,128)S(1)} %get-tuple-element.52), channel_id=1, source_target_pairs={{0,8},{8,16},{16,24},{1,9},{9,17},{17,25},{2,10},{10,18},{18,26},{... | collective-permute-start | bytes 49160 | tf_op jit(solution)/shard_map/ppermute | solution.py:20
  10.5 46.4 %all-to-all-start = ((bf16[4,2,4096]{2,1,0:T(2,128)(2,1)}), bf16[4,2,4096]{2,1,0:T(2,128)(2,1)S(1)}, u32[]{:S(2)}, u32[]{:S(2)}) async-start(bf16[4,2,4096]{2,1,0:T(2,128)(2,1)} %all_to_all.6), calls=%async_computation | async-start | bytes 131072 | tf_op jit(solution)/shard_map/all_to_all | solution.py:154
  29.9 61.0 %collective-permute-start.24 = (f32[1,8,64]{2,1,0:T(8,128)}, f32[1,8,64]{2,1,0:T(8,128)}, u32[]{:S(2)}, u32[]{:S(2)}) collective-permute-start(f32[1,8,64]{2,1,0:T(8,128)} %get-tuple-element.105), channel_id=1, source_target_pairs={{0,8},{8,16},{16,24},{1,9},{9,17},{17,25},{2,10},{10,18},{18,26},{... | collective-permute-start | bytes 6152 | tf_op jit(solution)/shard_map/ppermute | solution.py:20
  34.2 56.8 %collective-permute-start.25 = (f32[1,8,64]{2,1,0:T(8,128)}, f32[1,8,64]{2,1,0:T(8,128)}, u32[]{:S(2)}, u32[]{:S(2)}) collective-permute-start(f32[1,8,64]{2,1,0:T(8,128)} %get-tuple-element.106), channel_id=1, source_target_pairs={{8,0},{16,8},{24,16},{9,1},{17,9},{25,17},{10,2},{18,10},{26,18},{... | collective-permute-start | bytes 6152 | tf_op jit(solution)/shard_map/ppermute | solution.py:22
  43.7 8.4 %collective-permute-start.4 = (f32[20,20,2]{2,1,0:T(8,128)S(1)}, f32[20,20,2]{2,1,0:T(8,128)S(1)}, u32[]{:S(2)}, u32[]{:S(2)}) collective-permute-start(f32[20,20,2]{2,1,0:T(8,128)S(1)} %get-tuple-element.25), channel_id=1, source_target_pairs={{0,1},{1,2},{2,3},{4,5},{5,6},{6,7},{8,9},{9,10},{10,11},{12,13},{... | collective-permute-start | bytes 9608 | tf_op jit(solution)/shard_map/ppermute | solution.py:20
  49.0 7.5 %collective-permute-start.5 = (f32[20,20,2]{2,1,0:T(8,128)S(1)}, f32[20,20,2]{2,1,0:T(8,128)S(1)}, u32[]{:S(2)}, u32[]{:S(2)}) collective-permute-start(f32[20,20,2]{2,1,0:T(8,128)S(1)} %get-tuple-element.26), channel_id=1, source_target_pairs={{1,0},{2,1},{3,2},{5,4},{6,5},{7,6},{9,8},{10,9},{11,10},{13,12},{... | collective-permute-start | bytes 9608 | tf_op jit(solution)/shard_map/ppermute | solution.py:22
  58.6 6.3 %collective-permute-start.6 = (f32[1,16,128]{2,1,0:T(8,128)S(1)}, f32[1,16,128]{2,1,0:T(8,128)S(1)}, u32[]{:S(2)}, u32[]{:S(2)}) collective-permute-start(f32[1,16,128]{2,1,0:T(8,128)S(1)} %slice.1002), channel_id=1, source_target_pairs={{0,8},{8,16},{16,24},{1,9},{9,17},{17,25},{2,10},{10,18},{18,26},{... | collective-permute-start | bytes 24584 | tf_op jit(solution)/shard_map/ppermute | solution.py:20
  73.9 7.5 %collective-permute-start.10 = (f32[18,18,1]{2,1,0:T(8,128)S(1)}, f32[18,18,1]{2,1,0:T(8,128)S(1)}, u32[]{:S(2)}, u32[]{:S(2)}) collective-permute-start(f32[18,18,1]{2,1,0:T(8,128)S(1)} %get-tuple-element.29), channel_id=1, source_target_pairs={{0,1},{1,2},{2,3},{4,5},{5,6},{6,7},{8,9},{9,10},{10,11},{12,13},{... | collective-permute-start | bytes 3896 | tf_op jit(solution)/shard_map/ppermute | solution.py:20
  78.5 7.3 %collective-permute-start.11 = (f32[18,18,1]{2,1,0:T(8,128)S(1)}, f32[18,18,1]{2,1,0:T(8,128)S(1)}, u32[]{:S(2)}, u32[]{:S(2)}) collective-permute-start(f32[18,18,1]{2,1,0:T(8,128)S(1)} %get-tuple-element.30), channel_id=1, source_target_pairs={{1,0},{2,1},{3,2},{5,4},{6,5},{7,6},{9,8},{10,9},{11,10},{13,12},{... | collective-permute-start | bytes 3896 | tf_op jit(solution)/shard_map/ppermute | solution.py:22
  87.0 7.5 %collective-permute-start.12 = (f32[2,16,128]{2,1,0:T(8,128)S(1)}, f32[2,16,128]{2,1,0:T(8,128)S(1)}, u32[]{:S(2)}, u32[]{:S(2)}) collective-permute-start(f32[2,16,128]{2,1,0:T(8,128)S(1)} %get-tuple-element.49), channel_id=1, source_target_pairs={{0,8},{8,16},{16,24},{1,9},{9,17},{17,25},{2,10},{10,18},{18,26},{... | collective-permute-start | bytes 49160 | tf_op jit(solution)/shard_map/ppermute | solution.py:20
  91.9 17.4 %collective-permute-start.26 = (f32[10,1,64]{2,1,0:T(1,128)S(1)}, f32[10,1,64]{2,1,0:T(1,128)S(1)}, u32[]{:S(2)}, u32[]{:S(2)}) collective-permute-start(f32[10,1,64]{2,1,0:T(1,128)S(1)} %get-tuple-element.87), channel_id=1, source_target_pairs={{0,4},{1,5},{2,6},{3,7},{8,12},{9,13},{10,14},{11,15},{16,20},{17,... | collective-permute-start | bytes 7688 | tf_op jit(solution)/shard_map/ppermute | solution.py:20
  93.2 16.0 %collective-permute-start.27 = (f32[10,1,64]{2,1,0:T(1,128)S(1)}, f32[10,1,64]{2,1,0:T(1,128)S(1)}, u32[]{:S(2)}, u32[]{:S(2)}) collective-permute-start(f32[10,1,64]{2,1,0:T(1,128)S(1)} %get-tuple-element.88), channel_id=1, source_target_pairs={{4,0},{5,1},{6,2},{7,3},{12,8},{13,9},{14,10},{15,11},{20,16},{21,... | collective-permute-start | bytes 7688 | tf_op jit(solution)/shard_map/ppermute | solution.py:22
  94.6 6.1 %collective-permute-start.14 = (f32[20,2,128]{2,1,0:T(2,128)S(1)}, f32[20,2,128]{2,1,0:T(2,128)S(1)}, u32[]{:S(2)}, u32[]{:S(2)}) collective-permute-start(f32[20,2,128]{2,1,0:T(2,128)S(1)} %get-tuple-element.35), channel_id=1, source_target_pairs={{0,4},{1,5},{2,6},{3,7},{8,12},{9,13},{10,14},{11,15},{16,20},{17,... | collective-permute-start | bytes 61448 | tf_op jit(solution)/shard_map/ppermute | solution.py:20
  103.3 7.1 %collective-permute-start.16 = (f32[20,20,2]{2,1,0:T(8,128)S(1)}, f32[20,20,2]{2,1,0:T(8,128)S(1)}, u32[]{:S(2)}, u32[]{:S(2)}) collective-permute-start(f32[20,20,2]{2,1,0:T(8,128)S(1)} %get-tuple-element.23), channel_id=1, source_target_pairs={{0,1},{1,2},{2,3},{4,5},{5,6},{6,7},{8,9},{9,10},{10,11},{12,13},{... | collective-permute-start | bytes 9608 | tf_op jit(solution)/shard_map/ppermute | solution.py:20
  107.3 7.5 %collective-permute-start.17 = (f32[20,20,2]{2,1,0:T(8,128)S(1)}, f32[20,20,2]{2,1,0:T(8,128)S(1)}, u32[]{:S(2)}, u32[]{:S(2)}) collective-permute-start(f32[20,20,2]{2,1,0:T(8,128)S(1)} %get-tuple-element.24), channel_id=1, source_target_pairs={{1,0},{2,1},{3,2},{5,4},{6,5},{7,6},{9,8},{10,9},{11,10},{13,12},{... | collective-permute-start | bytes 9608 | tf_op jit(solution)/shard_map/ppermute | solution.py:22
  117.0 10.0 %collective-permute-start.18 = (f32[1,16,128]{2,1,0:T(8,128)S(1)}, f32[1,16,128]{2,1,0:T(8,128)S(1)}, u32[]{:S(2)}, u32[]{:S(2)}) collective-permute-start(f32[1,16,128]{2,1,0:T(8,128)S(1)} %get-tuple-element.47), channel_id=1, source_target_pairs={{0,8},{8,16},{16,24},{1,9},{9,17},{17,25},{2,10},{10,18},{18,26},{... | collective-permute-start | bytes 24584 | tf_op jit(solution)/shard_map/ppermute | solution.py:20
  122.7 17.1 %collective-permute-start.28 = (f32[10,10,1]{2,1,0:T(8,128)S(1)}, f32[10,10,1]{2,1,0:T(8,128)S(1)}, u32[]{:S(2)}, u32[]{:S(2)}) collective-permute-start(f32[10,10,1]{2,1,0:T(8,128)S(1)} %get-tuple-element.69), channel_id=1, source_target_pairs={{0,1},{1,2},{2,3},{4,5},{5,6},{6,7},{8,9},{9,10},{10,11},{12,13},{... | collective-permute-start | bytes 1208 | tf_op jit(solution)/shard_map/ppermute | solution.py:20
  124.7 15.1 %collective-permute-start.29 = (f32[10,10,1]{2,1,0:T(8,128)S(1)}, f32[10,10,1]{2,1,0:T(8,128)S(1)}, u32[]{:S(2)}, u32[]{:S(2)}) collective-permute-start(f32[10,10,1]{2,1,0:T(8,128)S(1)} %get-tuple-element.70), channel_id=1, source_target_pairs={{1,0},{2,1},{3,2},{5,4},{6,5},{7,6},{9,8},{10,9},{11,10},{13,12},{... | collective-permute-start | bytes 1208 | tf_op jit(solution)/shard_map/ppermute | solution.py:22
  133.0 7.6 %collective-permute-start.22 = (f32[18,18,1]{2,1,0:T(8,128)S(1)}, f32[18,18,1]{2,1,0:T(8,128)S(1)}, u32[]{:S(2)}, u32[]{:S(2)}) collective-permute-start(f32[18,18,1]{2,1,0:T(8,128)S(1)} %get-tuple-element.27), channel_id=1, source_target_pairs={{0,1},{1,2},{2,3},{4,5},{5,6},{6,7},{8,9},{9,10},{10,11},{12,13},{... | collective-permute-start | bytes 3896 | tf_op jit(solution)/shard_map/ppermute | solution.py:20
  137.7 7.3 %collective-permute-start.23 = (f32[18,18,1]{2,1,0:T(8,128)S(1)}, f32[18,18,1]{2,1,0:T(8,128)S(1)}, u32[]{:S(2)}, u32[]{:S(2)}) collective-permute-start(f32[18,18,1]{2,1,0:T(8,128)S(1)} %get-tuple-element.28), channel_id=1, source_target_pairs={{1,0},{2,1},{3,2},{5,4},{6,5},{7,6},{9,8},{10,9},{11,10},{13,12},{... | collective-permute-start | bytes 3896 | tf_op jit(solution)/shard_map/ppermute | solution.py:22
  173.9 6.5 %collective-permute-start.34 = (f32[10,10,1]{2,1,0:T(8,128)S(1)}, f32[10,10,1]{2,1,0:T(8,128)S(1)}, u32[]{:S(2)}, u32[]{:S(2)}) collective-permute-start(f32[10,10,1]{2,1,0:T(8,128)S(1)} %get-tuple-element.67), channel_id=1, source_target_pairs={{0,1},{1,2},{2,3},{4,5},{5,6},{6,7},{8,9},{9,10},{10,11},{12,13},{... | collective-permute-start | bytes 1208 | tf_op jit(solution)/shard_map/ppermute | solution.py:20
  178.5 5.8 %collective-permute-start.35 = (f32[10,10,1]{2,1,0:T(8,128)S(1)}, f32[10,10,1]{2,1,0:T(8,128)S(1)}, u32[]{:S(2)}, u32[]{:S(2)}) collective-permute-start(f32[10,10,1]{2,1,0:T(8,128)S(1)} %get-tuple-element.68), channel_id=1, source_target_pairs={{1,0},{2,1},{3,2},{5,4},{6,5},{7,6},{9,8},{10,9},{11,10},{13,12},{... | collective-permute-start | bytes 1208 | tf_op jit(solution)/shard_map/ppermute | solution.py:22
  196.8 6.6 %collective-permute-start.40 = (f32[10,10,1]{2,1,0:T(8,128)S(1)}, f32[10,10,1]{2,1,0:T(8,128)S(1)}, u32[]{:S(2)}, u32[]{:S(2)}) collective-permute-start(f32[10,10,1]{2,1,0:T(8,128)S(1)} %get-tuple-element.65), channel_id=1, source_target_pairs={{0,1},{1,2},{2,3},{4,5},{5,6},{6,7},{8,9},{9,10},{10,11},{12,13},{... | collective-permute-start | bytes 1208 | tf_op jit(solution)/shard_map/ppermute | solution.py:20
  201.5 5.8 %collective-permute-start.41 = (f32[10,10,1]{2,1,0:T(8,128)S(1)}, f32[10,10,1]{2,1,0:T(8,128)S(1)}, u32[]{:S(2)}, u32[]{:S(2)}) collective-permute-start(f32[10,10,1]{2,1,0:T(8,128)S(1)} %get-tuple-element.66), channel_id=1, source_target_pairs={{1,0},{2,1},{3,2},{5,4},{6,5},{7,6},{9,8},{10,9},{11,10},{13,12},{... | collective-permute-start | bytes 1208 | tf_op jit(solution)/shard_map/ppermute | solution.py:22
  219.3 9.7 %collective-permute-start.46 = (f32[10,10,1]{2,1,0:T(8,128)S(1)}, f32[10,10,1]{2,1,0:T(8,128)S(1)}, u32[]{:S(2)}, u32[]{:S(2)}) collective-permute-start(f32[10,10,1]{2,1,0:T(8,128)S(1)} %get-tuple-element.63), channel_id=1, source_target_pairs={{0,1},{1,2},{2,3},{4,5},{5,6},{6,7},{8,9},{9,10},{10,11},{12,13},{... | collective-permute-start | bytes 1208 | tf_op jit(solution)/shard_map/ppermute | solution.py:20
  224.0 5.8 %collective-permute-start.47 = (f32[10,10,1]{2,1,0:T(8,128)S(1)}, f32[10,10,1]{2,1,0:T(8,128)S(1)}, u32[]{:S(2)}, u32[]{:S(2)}) collective-permute-start(f32[10,10,1]{2,1,0:T(8,128)S(1)} %get-tuple-element.64), channel_id=1, source_target_pairs={{1,0},{2,1},{3,2},{5,4},{6,5},{7,6},{9,8},{10,9},{11,10},{13,12},{... | collective-permute-start | bytes 1208 | tf_op jit(solution)/shard_map/ppermute | solution.py:22
  226.0 8.6 %collective-permute-start.54 = (f32[1,4,32]{2,1,0:T(4,128)S(1)}, f32[1,4,32]{2,1,0:T(4,128)S(1)}, u32[]{:S(2)}, u32[]{:S(2)}) collective-permute-start(f32[1,4,32]{2,1,0:T(4,128)S(1)} %get-tuple-element.121), channel_id=1, source_target_pairs={{0,8},{8,16},{16,24},{1,9},{9,17},{17,25},{2,10},{10,18},{18,26},{... | collective-permute-start | bytes 1544 | tf_op jit(solution)/shard_map/ppermute | solution.py:20
  227.6 6.9 %collective-permute-start.55 = (f32[1,4,32]{2,1,0:T(4,128)S(1)}, f32[1,4,32]{2,1,0:T(4,128)S(1)}, u32[]{:S(2)}, u32[]{:S(2)}) collective-permute-start(f32[1,4,32]{2,1,0:T(4,128)S(1)} %get-tuple-element.122), channel_id=1, source_target_pairs={{8,0},{16,8},{24,16},{9,1},{17,9},{25,17},{10,2},{18,10},{26,18},{... | collective-permute-start | bytes 1544 | tf_op jit(solution)/shard_map/ppermute | solution.py:22
  229.9 7.3 %collective-permute-start.48 = (f32[1,8,64]{2,1,0:T(8,128)S(1)}, f32[1,8,64]{2,1,0:T(8,128)S(1)}, u32[]{:S(2)}, u32[]{:S(2)}) collective-permute-start(f32[1,8,64]{2,1,0:T(8,128)S(1)} %get-tuple-element.97), channel_id=1, source_target_pairs={{0,8},{8,16},{16,24},{1,9},{9,17},{17,25},{2,10},{10,18},{18,26},{... | collective-permute-start | bytes 6152 | tf_op jit(solution)/shard_map/ppermute | solution.py:20
  234.6 19.6 %collective-permute-start.56 = (f32[6,1,32]{2,1,0:T(1,128)S(1)}, f32[6,1,32]{2,1,0:T(1,128)S(1)}, u32[]{:S(2)}, u32[]{:S(2)}) collective-permute-start(f32[6,1,32]{2,1,0:T(1,128)S(1)} %get-tuple-element.115), channel_id=1, source_target_pairs={{0,4},{1,5},{2,6},{3,7},{8,12},{9,13},{10,14},{11,15},{16,20},{17,... | collective-permute-start | bytes 2312 | tf_op jit(solution)/shard_map/ppermute | solution.py:20
  235.9 18.2 %collective-permute-start.57 = (f32[6,1,32]{2,1,0:T(1,128)S(1)}, f32[6,1,32]{2,1,0:T(1,128)S(1)}, u32[]{:S(2)}, u32[]{:S(2)}) collective-permute-start(f32[6,1,32]{2,1,0:T(1,128)S(1)} %get-tuple-element.116), channel_id=1, source_target_pairs={{4,0},{5,1},{6,2},{7,3},{12,8},{13,9},{14,10},{15,11},{20,16},{21,... | collective-permute-start | bytes 2312 | tf_op jit(solution)/shard_map/ppermute | solution.py:22
  245.8 8.5 %collective-permute-start.52 = (f32[10,10,1]{2,1,0:T(8,128)S(1)}, f32[10,10,1]{2,1,0:T(8,128)S(1)}, u32[]{:S(2)}, u32[]{:S(2)}) collective-permute-start(f32[10,10,1]{2,1,0:T(8,128)S(1)} %get-tuple-element.61), channel_id=1, source_target_pairs={{0,1},{1,2},{2,3},{4,5},{5,6},{6,7},{8,9},{9,10},{10,11},{12,13},{... | collective-permute-start | bytes 1208 | tf_op jit(solution)/shard_map/ppermute | solution.py:20
  252.2 5.8 %collective-permute-start.53 = (f32[10,10,1]{2,1,0:T(8,128)S(1)}, f32[10,10,1]{2,1,0:T(8,128)S(1)}, u32[]{:S(2)}, u32[]{:S(2)}) collective-permute-start(f32[10,10,1]{2,1,0:T(8,128)S(1)} %get-tuple-element.62), channel_id=1, source_target_pairs={{1,0},{2,1},{3,2},{5,4},{6,5},{7,6},{9,8},{10,9},{11,10},{13,12},{... | collective-permute-start | bytes 1208 | tf_op jit(solution)/shard_map/ppermute | solution.py:22
  259.4 10.0 %collective-permute-start.60 = (f32[1,4,32]{2,1,0:T(4,128)S(1)}, f32[1,4,32]{2,1,0:T(4,128)S(1)}, u32[]{:S(2)}, u32[]{:S(2)}) collective-permute-start(f32[1,4,32]{2,1,0:T(4,128)S(1)} %get-tuple-element.123), channel_id=1, source_target_pairs={{0,8},{8,16},{16,24},{1,9},{9,17},{17,25},{2,10},{10,18},{18,26},{... | collective-permute-start | bytes 1544 | tf_op jit(solution)/shard_map/ppermute | solution.py:20
  265.0 16.9 %collective-permute-start.58 = (f32[6,6,1]{2,1,0:T(8,128)S(1)}, f32[6,6,1]{2,1,0:T(8,128)S(1)}, u32[]{:S(2)}, u32[]{:S(2)}) collective-permute-start(f32[6,6,1]{2,1,0:T(8,128)S(1)} %get-tuple-element.109), channel_id=1, source_target_pairs={{0,1},{1,2},{2,3},{4,5},{5,6},{6,7},{8,9},{9,10},{10,11},{12,13},{... | collective-permute-start | bytes 440 | tf_op jit(solution)/shard_map/ppermute | solution.py:20
  267.2 14.8 %collective-permute-start.59 = (f32[6,6,1]{2,1,0:T(8,128)S(1)}, f32[6,6,1]{2,1,0:T(8,128)S(1)}, u32[]{:S(2)}, u32[]{:S(2)}) collective-permute-start(f32[6,6,1]{2,1,0:T(8,128)S(1)} %get-tuple-element.110), channel_id=1, source_target_pairs={{1,0},{2,1},{3,2},{5,4},{6,5},{7,6},{9,8},{10,9},{11,10},{13,12},{... | collective-permute-start | bytes 440 | tf_op jit(solution)/shard_map/ppermute | solution.py:22
  275.2 7.6 %collective-permute-start.64 = (f32[6,6,1]{2,1,0:T(8,128)S(1)}, f32[6,6,1]{2,1,0:T(8,128)S(1)}, u32[]{:S(2)}, u32[]{:S(2)}) collective-permute-start(f32[6,6,1]{2,1,0:T(8,128)S(1)} %get-tuple-element.111), channel_id=1, source_target_pairs={{0,1},{1,2},{2,3},{4,5},{5,6},{6,7},{8,9},{9,10},{10,11},{12,13},{... | collective-permute-start | bytes 440 | tf_op jit(solution)/shard_map/ppermute | solution.py:20
  339.9 9.3 %collective-permute-start.70 = (f32[6,6,1]{2,1,0:T(8,128)S(1)}, f32[6,6,1]{2,1,0:T(8,128)S(1)}, u32[]{:S(2)}, u32[]{:S(2)}) collective-permute-start(f32[6,6,1]{2,1,0:T(8,128)S(1)} %get-tuple-element.107), channel_id=1, source_target_pairs={{0,1},{1,2},{2,3},{4,5},{5,6},{6,7},{8,9},{9,10},{10,11},{12,13},{... | collective-permute-start | bytes 440 | tf_op jit(solution)/shard_map/ppermute | solution.py:20
  407.0 9.3 %collective-permute-start.76 = (f32[10,10,1]{2,1,0:T(8,128)S(1)}, f32[10,10,1]{2,1,0:T(8,128)S(1)}, u32[]{:S(2)}, u32[]{:S(2)}) collective-permute-start(f32[10,10,1]{2,1,0:T(8,128)S(1)} %get-tuple-element.59), channel_id=1, source_target_pairs={{0,1},{1,2},{2,3},{4,5},{5,6},{6,7},{8,9},{9,10},{10,11},{12,13},{... | collective-permute-start | bytes 1208 | tf_op jit(solution)/shard_map/ppermute | solution.py:20
  414.3 5.8 %collective-permute-start.77 = (f32[10,10,1]{2,1,0:T(8,128)S(1)}, f32[10,10,1]{2,1,0:T(8,128)S(1)}, u32[]{:S(2)}, u32[]{:S(2)}) collective-permute-start(f32[10,10,1]{2,1,0:T(8,128)S(1)} %get-tuple-element.60), channel_id=1, source_target_pairs={{1,0},{2,1},{3,2},{5,4},{6,5},{7,6},{9,8},{10,9},{11,10},{13,12},{... | collective-permute-start | bytes 1208 | tf_op jit(solution)/shard_map/ppermute | solution.py:22
  433.1 6.4 %collective-permute-start.82 = (f32[10,10,1]{2,1,0:T(8,128)S(1)}, f32[10,10,1]{2,1,0:T(8,128)S(1)}, u32[]{:S(2)}, u32[]{:S(2)}) collective-permute-start(f32[10,10,1]{2,1,0:T(8,128)S(1)} %get-tuple-element.57), channel_id=1, source_target_pairs={{0,1},{1,2},{2,3},{4,5},{5,6},{6,7},{8,9},{9,10},{10,11},{12,13},{... | collective-permute-start | bytes 1208 | tf_op jit(solution)/shard_map/ppermute | solution.py:20
  457.3 6.6 %collective-permute-start.88 = (f32[10,10,1]{2,1,0:T(8,128)S(1)}, f32[10,10,1]{2,1,0:T(8,128)S(1)}, u32[]{:S(2)}, u32[]{:S(2)}) collective-permute-start(f32[10,10,1]{2,1,0:T(8,128)S(1)} %get-tuple-element.55), channel_id=1, source_target_pairs={{0,1},{1,2},{2,3},{4,5},{5,6},{6,7},{8,9},{9,10},{10,11},{12,13},{... | collective-permute-start | bytes 1208 | tf_op jit(solution)/shard_map/ppermute | solution.py:20
  479.8 6.9 %collective-permute-start.94 = (f32[10,10,1]{2,1,0:T(8,128)S(1)}, f32[10,10,1]{2,1,0:T(8,128)S(1)}, u32[]{:S(2)}, u32[]{:S(2)}) collective-permute-start(f32[10,10,1]{2,1,0:T(8,128)S(1)} %get-tuple-element.53), channel_id=1, source_target_pairs={{0,1},{1,2},{2,3},{4,5},{5,6},{6,7},{8,9},{9,10},{10,11},{12,13},{... | collective-permute-start | bytes 1208 | tf_op jit(solution)/shard_map/ppermute | solution.py:20
  507.0 7.8 %collective-permute-start.100 = (f32[20,20,2]{2,1,0:T(8,128)S(1)}, f32[20,20,2]{2,1,0:T(8,128)S(1)}, u32[]{:S(2)}, u32[]{:S(2)}) collective-permute-start(f32[20,20,2]{2,1,0:T(8,128)S(1)} %get-tuple-element.21), channel_id=1, source_target_pairs={{0,1},{1,2},{2,3},{4,5},{5,6},{6,7},{8,9},{9,10},{10,11},{12,13},{... | collective-permute-start | bytes 9608 | tf_op jit(solution)/shard_map/ppermute | solution.py:20
  511.7 7.5 %collective-permute-start.101 = (f32[20,20,2]{2,1,0:T(8,128)S(1)}, f32[20,20,2]{2,1,0:T(8,128)S(1)}, u32[]{:S(2)}, u32[]{:S(2)}) collective-permute-start(f32[20,20,2]{2,1,0:T(8,128)S(1)} %get-tuple-element.22), channel_id=1, source_target_pairs={{1,0},{2,1},{3,2},{5,4},{6,5},{7,6},{9,8},{10,9},{11,10},{13,12},{... | collective-permute-start | bytes 9608 | tf_op jit(solution)/shard_map/ppermute | solution.py:22
  534.7 7.7 %collective-permute-start.106 = (f32[20,20,2]{2,1,0:T(8,128)S(1)}, f32[20,20,2]{2,1,0:T(8,128)S(1)}, u32[]{:S(2)}, u32[]{:S(2)}) collective-permute-start(f32[20,20,2]{2,1,0:T(8,128)S(1)} %get-tuple-element.19), channel_id=1, source_target_pairs={{0,1},{1,2},{2,3},{4,5},{5,6},{6,7},{8,9},{9,10},{10,11},{12,13},{... | collective-permute-start | bytes 9608 | tf_op jit(solution)/shard_map/ppermute | solution.py:20
  539.3 7.5 %collective-permute-start.107 = (f32[20,20,2]{2,1,0:T(8,128)S(1)}, f32[20,20,2]{2,1,0:T(8,128)S(1)}, u32[]{:S(2)}, u32[]{:S(2)}) collective-permute-start(f32[20,20,2]{2,1,0:T(8,128)S(1)} %get-tuple-element.20), channel_id=1, source_target_pairs={{1,0},{2,1},{3,2},{5,4},{6,5},{7,6},{9,8},{10,9},{11,10},{13,12},{... | collective-permute-start | bytes 9608 | tf_op jit(solution)/shard_map/ppermute | solution.py:22
  (78 other events, 1132.2 us)
where the time goes:
time: 554 us; the launch traced here: 551 us
  starting transfers between devices  262 us (47%)
  waiting for transfers between devices  145 us (26%)
  blocking collectives  74.6 us (13%)
  other arithmetic  32.8 us (6%)
  local copies, waits for them, and re-layouts  31.5 us (6%)
    ppermute x54, starting transfers between devices, with_halo(): lax.ppermute(tail, axis, [(i, (i + 1) % count) for i in range(ends)])  175 us
    ppermute x54, waiting for transfers between devices, with_halo(): lax.ppermute(head, axis, [((i + 1) % count, i) for i in range(ends)])  140 us
    ppermute x54, starting transfers between devices, with_halo(): lax.ppermute(head, axis, [((i + 1) % count, i) for i in range(ends)])  82.2 us
    psum x2, blocking collectives, dot_pair(): return lax.psum((first_term, second_term), ('gx', 'gy', 'gz'))  74.6 us
    reshape x3, local copies, waits for them, and re-layouts, coarsen(): values.reshape(extent_first // 2, 2, extent_second // 2, 2, extent_third...  21.5 us
  transfers between devices with their start and end apart: 109, of which 50 were waited for; matrix products, arithmetic and copies ran while one was open for 5% of the time, Pallas kernels for 0%

commit v1 on v0

v1 whole, which is shorter than its diff:
```python
import functools

import jax
import jax.numpy as jnp
from jax import lax
from jax.experimental import pallas as pl
from jax.experimental.pallas import tpu as pltpu
from jax.sharding import PartitionSpec as P

BOX = 16
SEND = 2
W = 4
F32 = jnp.float32
MESH = pl.DeviceIdType.MESH
HIGH = lax.Precision.HIGHEST


def iota(shape, dim):
    return lax.broadcasted_iota(jnp.int32, shape, dim)


def up(v, axis):
    return pltpu.roll(v, 1, axis)


def down(v, axis):
    return pltpu.roll(v, v.shape[axis] - 1, axis)


class Level:
    def __init__(self, x, y, z):
        self.x, self.y, self.z = x, y, z
        self.xe, self.ye = x + 2 * W, y + 2 * W
        self.ze = 128 if z + 2 * W <= 128 else z + 128
        self.own = 128
        self.tiles = -(-self.xe // 16)
        self.shape = (self.xe, self.ye, self.ze)


def axis_info(axis, counts):
    me = lax.axis_index(axis)
    n = counts[axis]
    return me, n


def send_pair(axis, n, pairs, sends, recvs):
    me = lax.axis_index(axis)
    (low_src, low_dst), (high_src, high_dst) = pairs
    low = pltpu.make_async_remote_copy(
        low_src, low_dst, sends.at[0], recvs.at[0],
        device_id={axis: lax.rem(me + n - 1, n)}, device_id_type=MESH)
    high = pltpu.make_async_remote_copy(
        high_src, high_dst, sends.at[1], recvs.at[1],
        device_id={axis: lax.rem(me + 1, n)}, device_id_type=MESH)
    has_low, has_high = me > 0, me < n - 1

    @pl.when(has_low)
    def _():
        low.start()

    @pl.when(has_high)
    def _():
        high.start()

    def finish():
        @pl.when(has_low)
        def _():
            low.wait_send()
            high.wait_recv()

        @pl.when(has_high)
        def _():
            high.wait_send()
            low.wait_recv()

    return finish


def exchange(lv, v, bufs, counts):
    py, ly, pz, lz, sends, recvs = bufs
    own = (pl.ds(0, lv.y), pl.ds(0, lv.own))
    finish = send_pair(
        "gx", counts["gx"],
        ((v.at[(pl.ds(W, W),) + own], v.at[(pl.ds(lv.x + W, W),) + own]),
         (v.at[(pl.ds(lv.x, W),) + own], v.at[(pl.ds(0, W),) + own])),
        sends.at[0], recvs.at[0])
    yield
    finish()
    py[0] = v[:, 0:W, 0:lv.own]
    py[1] = v[:, lv.y - W : lv.y, 0:lv.own]
    finish = send_pair(
        "gy", counts["gy"], ((py.at[0], ly.at[0]), (py.at[1], ly.at[1])), sends.at[1], recvs.at[1])
    yield
    finish()
    v[:, lv.y : lv.y + W, 0:lv.own] = ly[0]
    v[:, lv.y + W : lv.ye, 0:lv.own] = ly[1]
    lane = iota((lv.ye, 128), 1)
    for tile in range(lv.tiles):
        packed = jnp.zeros((lv.ye, 128), F32)
        for k in range(min(16, lv.xe - 16 * tile)):
            plane = v[16 * tile + k, :, 0:128]
            if lv.z == 64:
                plane = jnp.where(lane >= 64, pltpu.roll(plane, 64, 1), plane)
            packed = jnp.where(lane // 8 == k, pltpu.roll(plane, (8 * k + W) % 128, 1), packed)
        pz[tile] = packed
    finish = send_pair("gz", counts["gz"], ((pz, lz.at[0]), (pz, lz.at[1])), sends.at[2], recvs.at[2])
    yield
    finish()
    edge = (lane < W) | (lane >= 128 - W)
    for tile in range(lv.tiles):
        both = jnp.where(lane % 8 >= W, lz[0, tile], lz[1, tile])
        for k in range(min(16, lv.xe - 16 * tile)):
            x = 16 * tile + k
            strip = jnp.where(edge, pltpu.roll(both, (256 - 8 * k - W) % 128, 1), 0.0)
            if lv.z == 64:
                v[x] = jnp.where(lane < 64, v[x], jnp.where(lane >= 128 - W, strip, pltpu.roll(strip, 64, 1)))
            else:
                v[x, :, lv.z : lv.z + 128] = strip
    yield


def gather(buf, sends, recvs, counts):
    at = {axis: lax.axis_index(axis) for axis in counts}
    prefix = {"gz": (at["gx"], at["gy"]), "gy": (at["gx"],), "gx": ()}
    base = 0
    for axis in ("gz", "gy", "gx"):
        me, n = at[axis], counts[axis]
        copies = []
        for k in range(1, n):
            block = buf.at[prefix[axis] + (me,)]
            copy = pltpu.make_async_remote_copy(
                block, block, sends.at[base + k - 1], recvs.at[base + k - 1],
                device_id={axis: lax.rem(me + k, n)}, device_id_type=MESH)
            copy.start()
            source = buf.at[prefix[axis] + (lax.rem(me + n - k, n),)]
            arrive = pltpu.make_async_remote_copy(
                source, source, sends.at[base + k - 1], recvs.at[base + k - 1],
                device_id={axis: lax.rem(me + k, n)}, device_id_type=MESH)
            copies.append((copy, arrive))
        yield
        for copy, arrive in copies:
            copy.wait_send()
            arrive.wait_recv()
        base += n - 1
    yield


def together(*steps):
    for _ in zip(*steps):
        pass


def prepare(lv, k, fx, fy, fz, dd, iv):
    def body(x, carry):
        kx = k[x]
        below = 0.5 * (k[jnp.maximum(x - 1, 0)] + kx)
        above = 0.5 * (kx + k[jnp.minimum(x + 1, lv.xe - 1)])
        second = 0.5 * (up(kx, 0) + kx)
        third = 0.5 * (up(kx, 1) + kx)
        total = below + above + second + down(second, 0) + third + down(third, 1)
        fx[x], fy[x], fz[x], dd[x] = below, second, third, total
        iv[x] = jnp.where(kx > 0.0, 1.0 / total, 0.0)
        return carry

    lax.fori_loop(0, lv.xe, body, 0)


def around(v, x, mid, faces):
    fx, fy, fz = faces
    second, third = fy[x], fz[x]
    summed = fx[x] * v[x - 1] + fx[x + 1] * v[x + 1]
    summed = summed + second * up(mid, 0) + down(second * mid, 0)
    return summed + third * up(mid, 1) + down(third * mid, 1)


def half_sweep(lv, v, g, faces, iv, colour, batch):
    parity = iota((lv.ye, lv.ze), 0) + iota((lv.ye, lv.ze), 1)

    def body(step, carry):
        fresh = []
        for k in range(batch):
            x = 1 + step * batch + k
            mid = v[x]
            value = (g[x] + around(v, x, mid, faces)) * iv[x]
            fresh.append((x, jnp.where((parity + x) % 2 == colour, value, mid)))
        for x, value in fresh:
            v[x] = value
        return carry

    lax.fori_loop(0, (lv.xe - 2) // batch, body, 0)


def residual_pairs(lv, v, g, faces, dd, pairs):
    def body(i, carry):
        total = jnp.zeros((lv.ye, lv.ze), F32)
        for k in range(2):
            x = W + 2 * i + k
            mid = v[x]
            total = total + (g[x] - dd[x] * mid + around(v, x, mid, faces))
        pairs[i] = total[0 : lv.y, 0 : lv.own]
        return carry

    lax.fori_loop(0, lv.x // 2, body, 0)


def open_halo(lv, p, v, g, dd):
    parity = iota((lv.ye, lv.ze), 0) + iota((lv.ye, lv.ze), 1)

    def body(x, carry):
        red = (parity + x) % 2 == 0
        px = p[x]
        v[x] = jnp.where(red, px, 0.0)
        g[x] = jnp.where(red, px * dd[x], px)
        return carry

    lax.fori_loop(0, lv.xe, body, 0)


def fold_rows(pairs, rows):
    return pairs[:, pl.ds(0, rows, stride=2), :] + pairs[:, pl.ds(1, rows, stride=2), :]


def dot(a, b):
    return jnp.dot(a, b, precision=HIGH, preferred_element_type=F32)


def coarse_mid(pairs, x, y):
    folded = fold_rows(pairs, y // 2).reshape((x // 2) * (y // 2), 128)
    matrix = jnp.where(iota((128, 128), 0) // 2 == iota((128, 128), 1), 0.125, 0.0).astype(F32)
    return dot(folded, matrix).reshape(x // 2, y // 2, 128)


def coarse_low(pairs, count, rows, lanes, tmp, target):
    total = jnp.zeros((rows, 128), F32)
    source, goal = iota((128, 128), 0), iota((128, 128), 1)
    for x in range(count):
        matrix = jnp.where((source // 2 + x * lanes == goal) & (source < 2 * lanes), 0.125, 0.0).astype(F32)
        total = total + dot(pairs[x], matrix)
    tmp[...] = total
    half = rows // 2
    small = tmp[pl.ds(0, half, stride=2), :] + tmp[pl.ds(1, half, stride=2), :]
    target[0:half, :] = small
    target[half:rows, :] = small


def spread_low(buf, whole, counts, pad):
    lane, row = iota((8, 128), 1), iota((8, 128), 0)

    def body(a, carry):
        for i in range(4):
            for ct in range(counts["gy"] // 2):
                for gt in range(counts["gz"] // 4):
                    total = jnp.zeros((8, 128), F32)
                    for c in range(2):
                        for g in range(4):
                            piece = pltpu.roll(buf[a, 2 * ct + c, 4 * gt + g], (32 * (g - i)) % 128, 1)
                            total = jnp.where((lane // 32 == g) & (row // 4 == c), piece, total)
                    whole[pad + 4 * a + i, 8 * ct : 8 * ct + 8, 128 * gt : 128 * gt + 128] = total
        return carry

    lax.fori_loop(0, counts["gx"], body, 0)


def bottom(f, k, s, vv, xs, dims):
    planes, rows, lanes = dims
    row, lane = iota((rows, lanes), 0), iota((rows, lanes), 1)
    edges = (row > 0, row < rows - 1, lane > 0, lane < lanes - 1)

    def shifted(v):
        return (
            jnp.where(edges[0], up(v, 0), 0.0), jnp.where(edges[1], down(v, 0), 0.0),
            jnp.where(edges[2], up(v, 1), 0.0), jnp.where(edges[3], down(v, 1), 0.0))

    def operate(v, x):
        kx, mid = k[x], v[x]
        summed, diagonal = jnp.zeros_like(mid), jnp.zeros_like(mid)
        others = ((k[x - 1], v[x - 1]), (k[x + 1], v[x + 1])) + tuple(zip(shifted(kx), shifted(mid)))
        for other, value in others:
            face = 0.5 * (kx + other)
            diagonal = diagonal + face
            summed = summed + face * value
        return mid, (diagonal * mid - summed) * 0.0625

    zero = jnp.zeros((rows, lanes), F32)

    def first(x, carry):
        mid, image = operate(f, x + 1)
        vv[x] = image
        return carry[0] + mid * mid, carry[1] + mid * image

    def total(v):
        return jnp.sum(jnp.sum(v, axis=0, keepdims=True), axis=1, keepdims=True)

    norm, along = lax.fori_loop(0, planes, first, (zero, zero))
    alpha = total(norm) / total(along)

    def rest(x, carry):
        s[x + 1] = f[x + 1] - alpha * vv[x]
        return carry

    lax.fori_loop(0, planes, rest, 0)

    def second(x, carry):
        mid, image = operate(s, x + 1)
        return carry[0] + image * mid, carry[1] + image * image

    turned, norm = lax.fori_loop(0, planes, second, (zero, zero))
    omega = total(turned) / total(norm)

    def join(x, carry):
        xs[x + 2] = alpha * f[x + 1] + omega * s[x + 1]
        return carry

    lax.fori_loop(0, planes, join, 0)


def pack_boxes(slots, ids, outgoing, boxes, groups):
    held = ids[0].astype(F32)
    cap = held.shape[1]
    eye = iota((cap, cap), 0) == iota((cap, cap), 1)
    rows = jnp.broadcast_to(held, (cap, cap))
    cols = jnp.broadcast_to(jnp.sum(jnp.where(eye, rows, 0.0), axis=1, keepdims=True), (cap, cap))

    def target(v):
        return jnp.floor((v + 0.5) * (1.0 / boxes))

    earlier = (target(rows) == target(cols)) & (cols < rows) & (cols >= 0.0)
    ranking = jnp.sum(jnp.where(earlier, 1.0, 0.0), axis=0, keepdims=True)
    send_row = jnp.where(held >= 0.0, target(held) * SEND + ranking, -1.0)
    count = groups * SEND
    picker = jnp.where(iota((count, cap), 0).astype(F32) == jnp.broadcast_to(send_row, (count, cap)), 1.0, 0.0)
    data = slots[0, 0].astype(F32)
    total = jnp.zeros((count, data.shape[1]), F32)
    for q in range(cap):
        total = total + picker[:, q : q + 1] * data[q : q + 1, :]
    for t in range(groups):
        outgoing[t] = total[SEND * t : SEND * t + SEND, :]


def place_boxes(incoming, owner, lhs, rhs, boxes, groups):
    me = lax.axis_index("gz")
    owners = jnp.broadcast_to(owner[0].astype(F32), (boxes, owner.shape[2]))
    here = iota(owners.shape, 1) == iota(owners.shape, 0) + me * boxes
    col = jnp.sum(jnp.where(here, owners, 0.0), axis=1, keepdims=True)
    cols = jnp.broadcast_to(col, (boxes, boxes))
    first, second = iota((boxes, boxes), 0), iota((boxes, boxes), 1)
    row = jnp.sum(jnp.where(first == second, cols, 0.0), axis=0, keepdims=True)
    before = (jnp.broadcast_to(row, (boxes, boxes)) == cols) & (second < first)
    pick = col * SEND + jnp.sum(jnp.where(before, 1.0, 0.0), axis=1, keepdims=True)
    face = BOX * BOX
    mine = iota((BOX, face), 1) // BOX == iota((BOX, face), 0)
    for i in range(BOX):
        chosen = jnp.zeros((boxes, face), F32)
        for r in range(groups * SEND):
            chosen = jnp.where(pick == float(r), incoming[r // SEND, r % SEND : r % SEND + 1, face * i : face * i + face], chosen)
        for b in range(boxes):
            piece = jnp.where(mine, jnp.broadcast_to(chosen[b : b + 1, :], (BOX, face)), 0.0)
            lhs[BOX * i : BOX * i + BOX, face * b : face * b + face] = piece.astype(jnp.bfloat16)
    return jnp.dot(lhs[...], rhs[...], preferred_element_type=F32)


def kernel(fine, mid, counts, names, slots, ids, owner, coef, out, *scratch):
    r = dict(zip(names, scratch))
    groups = counts["gz"]
    boxes = fine.z // BOX
    at = {axis: lax.axis_index(axis) for axis in counts}
    for name in ("K0", "P0", "Q0", "K1", "P1", "E1", "ly", "lz", "lym", "lzm", "f2", "k2", "s2", "x2"):
        r[name][...] = jnp.zeros(r[name].shape, F32)

    barrier = pltpu.get_barrier_semaphore()
    for axis, n in counts.items():
        for k in range(1, n):
            pl.semaphore_signal(
                barrier, inc=1, device_id={axis: lax.rem(at[axis] + k, n)}, device_id_type=MESH)

    pack_boxes(slots, ids, r["outgoing"], boxes, groups)
    K0, K1 = r["K0"], r["K1"]
    K0[W : W + fine.x, 0 : fine.y, 0:128] = coef[...]
    for i in range(mid.x):
        r["pairs"][i] = coef[2 * i] + coef[2 * i + 1]
    K1[W : W + mid.x, 0 : mid.y, :] = coarse_mid(r["pairs"], fine.x, fine.y)
    for i in range(mid.x // 2):
        r["pairsm"][i] = K1[W + 2 * i, 0 : mid.y, :] + K1[W + 2 * i + 1, 0 : mid.y, :]
    here = (at["gx"], at["gy"], at["gz"])
    coarse_low(r["pairsm"], mid.x // 2, mid.y, mid.z // 2, r["tmp"], r["gk"].at[here])
    pl.semaphore_wait(barrier, sum(counts.values()) - len(counts))

    moves = []
    me = at["gz"]
    for k in range(1, groups):
        to, source = lax.rem(me + k, groups), lax.rem(me + groups - k, groups)
        copy = pltpu.make_async_remote_copy(
            r["outgoing"].at[to], r["incoming"].at[me], r["ms"].at[k - 1], r["mr"].at[k - 1],
            device_id={"gz": to}, device_id_type=MESH)
        copy.start()
        arrive = pltpu.make_async_remote_copy(
            r["outgoing"].at[to], r["incoming"].at[source], r["ms"].at[k - 1], r["mr"].at[k - 1],
            device_id={"gz": to}, device_id_type=MESH)
        moves.append((copy, arrive))
    r["incoming"][me] = r["outgoing"][me]

    def bufs(n, tail):
        return tuple(r[b + tail].at[n] for b in ("py", "ly", "pz", "lz", "es", "er"))

    steps = [
        exchange(fine, K0, bufs(0, ""), counts), exchange(mid, K1, bufs(0, "m"), counts),
        gather(r["gk"], r["gs"].at[0], r["gr"].at[0], counts)]
    for step in steps:
        next(step)
    lane = iota((BOX * BOX, 128), 1)
    folded = iota((BOX * BOX, 128), 0) % BOX == lane % BOX
    for b in range(boxes):
        block = jnp.where(folded & (lane // BOX == b), 1.0, 0.0)
        r["rhs"][BOX * BOX * b : BOX * BOX * (b + 1), :] = block.astype(jnp.bfloat16)
    for copy, arrive in moves:
        copy.wait_send()
        arrive.wait_recv()
    source = place_boxes(r["incoming"], owner, r["lhs"], r["rhs"], boxes, groups)
    source = source.reshape(fine.x, fine.y, 128)
    together(*steps)

    faces0 = (r["fx0"], r["fy0"], r["fz0"])
    faces1 = (r["fx1"], r["fy1"], r["fz1"])
    dd0, iv0, dd1, iv1 = r["dd0"], r["iv0"], r["dd1"], r["iv1"]
    v0, g0, v1, g1 = r["v0"], r["g0"], r["v1"], r["g1"]
    prepare(fine, K0, *faces0, dd0, iv0)
    parity = iota((fine.y, 128), 0) + iota((fine.y, 128), 1)
    for x in range(fine.x):
        red = (parity + x) % 2 == 0
        r["P0"][W + x, 0 : fine.y, 0:128] = jnp.where(red, source[x] * iv0[W + x, 0 : fine.y, 0:128], source[x])
    step = exchange(fine, r["P0"], bufs(1, ""), counts)
    next(step)
    prepare(mid, K1, *faces1, dd1, iv1)
    together(step)
    open_halo(fine, r["P0"], v0, g0, dd0)
    for colour in (1, 0, 1):
        half_sweep(fine, v0, g0, faces0, iv0, colour, 2)
    residual_pairs(fine, v0, g0, faces0, dd0, r["pairs"])

    source1 = coarse_mid(r["pairs"], fine.x, fine.y)
    parity = iota((mid.y, 128), 0) + iota((mid.y, 128), 1)
    for x in range(mid.x):
        red = (parity + x) % 2 == 0
        scaled = 4.0 * source1[x]
        r["P1"][W + x, 0 : mid.y, :] = jnp.where(red, scaled * iv1[W + x, 0 : mid.y, :], scaled)
    step = exchange(mid, r["P1"], bufs(1, "m"), counts)
    next(step)
    spread_low(r["gk"], r["k2"], counts, 1)
    together(step)
    open_halo(mid, r["P1"], v1, g1, dd1)
    for colour in (1, 0, 1):
        half_sweep(mid, v1, g1, faces1, iv1, colour, 2)
    residual_pairs(mid, v1, g1, faces1, dd1, r["pairsm"])
    for i in range(mid.x // 2):
        r["pairsm"][i] = r["pairsm"][i] * 0.25
    coarse_low(r["pairsm"], mid.x // 2, mid.y, mid.z // 2, r["tmp"], r["gf"].at[here])
    r["E1"][W : W + mid.x, 0 : mid.y, :] = v1[W : W + mid.x, 0 : mid.y, :]
    together(
        gather(r["gf"], r["gs"].at[1], r["gr"].at[1], counts),
        exchange(mid, r["E1"], bufs(2, "m"), counts))

    planes, rows, lanes = 4 * counts["gx"], 4 * counts["gy"], 32 * counts["gz"]
    spread_low(r["gf"], r["f2"], counts, 1)
    bottom(r["f2"], r["k2"], r["s2"], r["v2"], r["x2"], (planes, rows, lanes))
    row8 = iota((8, lanes), 0)
    for q in range(8):
        plane = r["x2"][4 * at["gx"] + q]
        turned = plane
        for c in range(1, counts["gy"]):
            turned = jnp.where(at["gy"] == c, pltpu.roll(plane, rows - 4 * c, 0), turned)
        r["local"][q] = jnp.where(row8 < 6, turned[0:8, :], turned[rows - 8 : rows, :])
    goal = iota((lanes, 128), 1)
    cell = jnp.where(goal < mid.z + W, goal, goal - 128)
    cell = (cell + 128) // 2 - 64
    wanted = (goal < mid.z + W) | (goal >= 128 - W)
    matrix = jnp.where((iota((lanes, 128), 0) == 32 * at["gz"] + cell) & wanted, 1.0, 0.0).astype(F32)
    spread = dot(r["local"][...].reshape(64, lanes), matrix).reshape(8, 8, 128)
    E1 = r["E1"]
    for q in range(8):
        r["wide"][pl.ds(0, 8, stride=2), :] = spread[q]
        r["wide"][pl.ds(1, 8, stride=2), :] = spread[q]
        for k in range(2):
            x = 2 * q + k
            E1[x] = jnp.where(K1[x] > 0.0, E1[x] + r["wide"][...], 0.0)
    for colour in (0, 1, 0, 1):
        half_sweep(mid, E1, g1, faces1, iv1, colour, 2)

    matrix = jnp.where(iota((128, 128), 0) == iota((128, 128), 1) // 2, 1.0, 0.0).astype(F32)
    fresh = dot(E1[W : W + mid.x, 0 : mid.y, :].reshape(mid.x * mid.y, 128), matrix).reshape(mid.x, mid.y, 128)
    Q0 = r["Q0"]
    for i in range(mid.x):
        r["wide"][pl.ds(0, mid.y, stride=2), :] = fresh[i]
        r["wide"][pl.ds(1, mid.y, stride=2), :] = fresh[i]
        for k in range(2):
            x = W + 2 * i + k
            Q0[x, 0 : fine.y, 0:128] = v0[x, 0 : fine.y, 0:128] + r["wide"][...]
    together(exchange(fine, Q0, bufs(2, ""), counts))
    for colour in (0, 1, 0, 1):
        half_sweep(fine, Q0, g0, faces0, iv0, colour, 2)
    out[...] = Q0[W : W + fine.x, 0 : fine.y, 0:128]


def per_device(counts, old_slots, old_ids, old_owner, coefficient):
    x, y, z = coefficient.shape
    fine, mid = Level(x, y, z), Level(x // 2, y // 2, z // 2)
    planes, rows, lanes = 4 * counts["gx"], 4 * counts["gy"], 32 * counts["gz"]
    groups, boxes = counts["gz"], z // BOX
    cells = old_slots.shape[3]
    partners = sum(counts.values()) - len(counts)
    vmem = lambda *shape: pltpu.VMEM(shape, F32)
    dma = lambda *shape: pltpu.SemaphoreType.DMA(shape)
    scratch = {}
    for level, tail, names in ((fine, "", ("K0", "P0", "Q0")), (mid, "m", ("K1", "P1", "E1"))):
        for name in names:
            scratch[name] = vmem(*level.shape)
        scratch["py" + tail] = vmem(3, 2, level.xe, W, 128)
        scratch["ly" + tail] = vmem(3, 2, level.xe, W, 128)
        scratch["pz" + tail] = vmem(3, level.tiles, level.ye, 128)
        scratch["lz" + tail] = vmem(3, 2, level.tiles, level.ye, 128)
        scratch["es" + tail] = dma(3, 3, 2)
        scratch["er" + tail] = dma(3, 3, 2)
        scratch["pairs" + tail] = vmem(level.x // 2, level.y, 128)
    for level, tail in ((fine, "0"), (mid, "1")):
        for name in ("fx", "fy", "fz", "dd", "iv", "v", "g"):
            scratch[name + tail] = vmem(*level.shape)
    scratch.update(
        outgoing=vmem(groups, SEND, cells), incoming=vmem(groups, SEND, cells), ms=dma(groups - 1), mr=dma(groups - 1),
        lhs=pltpu.VMEM((BOX * BOX, boxes * BOX * BOX), jnp.bfloat16),
        rhs=pltpu.VMEM((boxes * BOX * BOX, 128), jnp.bfloat16),
        tmp=vmem(mid.y, 128), wide=vmem(16, 128), local=vmem(8, 8, lanes),
        gk=vmem(counts["gx"], counts["gy"], groups, 8, 128), gf=vmem(counts["gx"], counts["gy"], groups, 8, 128),
        gs=dma(2, partners), gr=dma(2, partners),
        f2=vmem(planes + 2, rows, lanes), k2=vmem(planes + 2, rows, lanes), s2=vmem(planes + 2, rows, lanes),
        v2=vmem(planes, rows, lanes), x2=vmem(planes + 4, rows, lanes))
    return pl.pallas_call(
        functools.partial(kernel, fine, mid, counts, tuple(scratch)),
        out_shape=jax.ShapeDtypeStruct(coefficient.shape, F32),
        in_specs=[pl.BlockSpec(memory_space=pltpu.VMEM)] * 4,
        out_specs=pl.BlockSpec(memory_space=pltpu.VMEM),
        scratch_shapes=list(scratch.values()),
        compiler_params=pltpu.CompilerParams(
            collective_id=0, has_side_effects=True, vmem_limit_bytes=60 * 1024 * 1024),
    )(old_slots, old_ids, old_owner, coefficient)


def solution(mesh):
    counts = {axis: mesh.shape[axis] for axis in ("gx", "gy", "gz")}
    return jax.shard_map(
        functools.partial(per_device, counts), mesh=mesh,
        in_specs=(P("gx", "gy", "gz", None), P("gx", "gy", "gz"), P("gx", "gy", None), P("gx", "gy", "gz")),
        out_specs=P("gx", "gy", "gz"), check_vma=False)
```

time: 554 us -> 77.5 us (0.14)
  starting transfers between devices: 262 us -> 0 us
  waiting for transfers between devices: 145 us -> 0 us
  Pallas kernels: 0 us -> 75.8 us
  blocking collectives: 74.6 us -> 0 us
  other arithmetic: 32.8 us -> 0 us
  local copies, waits for them, and re-layouts: 31.5 us -> 1.57 us
    ppermute x108 -> x0, starting transfers between devices: 257 us -> none  [the longest x54 175 us: with_halo(): lax.ppermute(tail, axis, [(i, (i + 1) % count) for i in range(ends)])]
    ppermute x108 -> x0, waiting for transfers between devices: 145 us -> none  [the longest x54 140 us: with_halo(): lax.ppermute(head, axis, [((i + 1) % count, i) for i in range(ends)])]
    pallas_call x0 -> x1, Pallas kernels: none -> 75.8 us  [per_device(): pl.pallas_call(functools.partial(kernel, fine, mid, counts, tuple(scratch...]
    psum x2 -> x0, blocking collectives: 74.6 us -> none  [dot_pair(): return lax.psum((first_term, second_term), ('gx', 'gy', 'gz'))]
    reshape x8 -> x0, local copies, waits for them, and re-layouts: 24.1 us -> none  [the longest x3 21.5 us: coarsen(): values.reshape(extent_first // 2, 2, extent_second // 2, 2, extent_third...]
    select_n x19 -> x0, other arithmetic: 11.8 us -> none  [the longest x14 9.6 us: relax(): return jnp.where(chosen, fresh, inner(padded))]
    reduce_sum x8 -> x0, other arithmetic: 11 us -> none  [the longest x4 8.39 us: coarsen(): return grouped.mean(axis=(1, 3, 5))]
  transfers between devices with their start and end apart: 109 -> 0, of which waited for: 50 -> 0; matrix products, arithmetic and copies ran while one was open for 5% -> 0% of each run, Pallas kernels for 0% -> 0%
where the time goes in v1:
time: 77.5 us; the launch traced here: 77.3 us
  Pallas kernels  75.8 us (98%)
  local copies, waits for them, and re-layouts  1.57 us (2%)
    pallas_call x1, Pallas kernels, per_device(): pl.pallas_call(functools.partial(kernel, fine, mid, counts, tuple(scratch...  75.8 us
    unnamed x1, local copies, waits for them, and re-layouts  1.57 us

profile of v1, /device:TPU:1, one launch (start us, length us, event | category | flops | bytes accessed | tf_op | source)
XLA Modules:
  0.0 77.3 jit_solution(5861116129190209637)
XLA Ops:
  0.0 75.8 %shard_map.46 = f32[16,16,128]{2,1,0:T(8,128)} custom-call(bf16[1,1,8,4096]{3,2,1,0:T(8,128)(2,1)} %slots.1, s32[1,1,8]{2,1,0:T(1,128)} %ids.1, s32[1,1,32]{2,1,0:T(1,128)} %owner.1, f32[16,16,128]{2,1,0:T(8,128)} %coef.1), custom_call_target="tpu_custom_call" | custom-call | tf_op jit(solution)/shard_map/pallas_call | solution.py:535
  75.8 1.6 %copy.6 = f32[16,16,128]{2,1,0:T(8,128)} copy(f32[16,16,128]{2,1,0:T(8,128)} %shard_map.46) | data formatting | bytes 262144

commit v2 on v1

--- a/solution.py
+++ b/solution.py
@@ -32,137 +32,146 @@
         self.x, self.y, self.z = x, y, z
         self.xe, self.ye = x + 2 * W, y + 2 * W
         self.ze = 128 if z + 2 * W <= 128 else z + 128
-        self.own = 128
-        self.tiles = -(-self.xe // 16)
         self.shape = (self.xe, self.ye, self.ze)
 
 
-def axis_info(axis, counts):
-    me = lax.axis_index(axis)
-    n = counts[axis]
-    return me, n
-
-
-def send_pair(axis, n, pairs, sends, recvs):
-    me = lax.axis_index(axis)
-    (low_src, low_dst), (high_src, high_dst) = pairs
-    low = pltpu.make_async_remote_copy(
-        low_src, low_dst, sends.at[0], recvs.at[0],
-        device_id={axis: lax.rem(me + n - 1, n)}, device_id_type=MESH)
-    high = pltpu.make_async_remote_copy(
-        high_src, high_dst, sends.at[1], recvs.at[1],
-        device_id={axis: lax.rem(me + 1, n)}, device_id_type=MESH)
-    has_low, has_high = me > 0, me < n - 1
-
-    @pl.when(has_low)
-    def _():
-        low.start()
-
-    @pl.when(has_high)
-    def _():
-        high.start()
-
-    def finish():
-        @pl.when(has_low)
-        def _():
-            low.wait_send()
-            high.wait_recv()
-
-        @pl.when(has_high)
-        def _():
-            high.wait_send()
-            low.wait_recv()
-
-    return finish
+NEAR = [(a, b, c) for c in (-1, 0, 1) for b in (-1, 0, 1) for a in (-1, 0, 1) if (a, b, c) != (0, 0, 0)]
+
+
+def near(offset, counts):
+    target, exists = {}, None
+    for axis, step in zip(("gx", "gy", "gz"), offset):
+        me, n = lax.axis_index(axis), counts[axis]
+        if step:
+            target[axis] = lax.rem(me + step + n, n)
+            inside = me > 0 if step < 0 else me < n - 1
+            exists = inside if exists is None else jnp.logical_and(exists, inside)
+    return target, exists
 
 
 def exchange(lv, v, bufs, counts):
     py, ly, pz, lz, sends, recvs = bufs
-    own = (pl.ds(0, lv.y), pl.ds(0, lv.own))
-    finish = send_pair(
-        "gx", counts["gx"],
-        ((v.at[(pl.ds(W, W),) + own], v.at[(pl.ds(lv.x + W, W),) + own]),
-         (v.at[(pl.ds(lv.x, W),) + own], v.at[(pl.ds(0, W),) + own])),
-        sends.at[0], recvs.at[0])
+    own = slice(W, W + lv.x)
+    py[0] = v[own, 0:W, 0:128]
+    py[1] = v[own, lv.y - W : lv.y, 0:128]
+    lane = iota((lv.y, 128), 1)
+    packed = jnp.zeros((lv.y, 128), F32)
+    for k in range(lv.x):
+        plane = v[W + k, 0 : lv.y, 0:128]
+        if lv.z == 64:
+            plane = jnp.where(lane >= 64, pltpu.roll(plane, 64, 1), plane)
+        packed = jnp.where(lane // 8 == k, pltpu.roll(plane, (8 * k + W) % 128, 1), packed)
+    pz[...] = packed
+    block = (pl.ds(0, lv.y), pl.ds(0, 128))
+    taken = {-1: (0, W), 0: (0, lv.x), 1: (lv.x - W, W)}
+    landed = {-1: lv.x + W, 0: W, 1: 0}
+    copies = []
+    for at, (a, b, c) in enumerate(NEAR):
+        target, exists = near((a, b, c), counts)
+        first, count = taken[a]
+        if c:
+            src, dst = pz, lz.at[(1 - c) // 2, 1 - a, 1 - b]
+        elif b:
+            side = (b + 1) // 2
+            src, dst = py.at[side, pl.ds(first, count)], ly.at[side, pl.ds(landed[a], count)]
+        else:
+            src, dst = v.at[(pl.ds(W + first, count),) + block], v.at[(pl.ds(landed[a], count),) + block]
+        copy = pltpu.make_async_remote_copy(
+            src, dst, sends.at[at], recvs.at[at], device_id=target, device_id_type=MESH)
+        copies.append(((a, b, c), copy, exists))
+    for _, copy, exists in reversed(copies):
+        pl.when(exists)(copy.start)
     yield
-    finish()
-    py[0] = v[:, 0:W, 0:lv.own]
-    py[1] = v[:, lv.y - W : lv.y, 0:lv.own]
-    finish = send_pair(
-        "gy", counts["gy"], ((py.at[0], ly.at[0]), (py.at[1], ly.at[1])), sends.at[1], recvs.at[1])
-    yield
-    finish()
-    v[:, lv.y : lv.y + W, 0:lv.own] = ly[0]
-    v[:, lv.y + W : lv.ye, 0:lv.own] = ly[1]
-    lane = iota((lv.ye, 128), 1)
-    for tile in range(lv.tiles):
-        packed = jnp.zeros((lv.ye, 128), F32)
-        for k in range(min(16, lv.xe - 16 * tile)):
-            plane = v[16 * tile + k, :, 0:128]
+    for (a, b, c), copy, exists in copies:
+        pl.when(exists)(copy.wait_send)
+        pl.when(near((-a, -b, -c), counts)[1])(copy.wait_recv)
+    v[:, lv.y : lv.y + W, 0:128] = ly[0]
+    v[:, lv.y + W : lv.ye, 0:128] = ly[1]
+    row = iota((8, 128), 0)
+    side = iota((lv.ye, 128), 1)
+    edge = (side < W) | (side >= 128 - W)
+    for a in range(3):
+        parts = []
+        for c in range(2):
+            ends = jnp.where(row < W, lz[c, a, 2, 0:8, :], lz[c, a, 0, lv.y - 8 : lv.y, :])
+            parts.append(jnp.concatenate([lz[c, a, 1], ends], axis=0))
+        both = jnp.where(side % 8 >= W, parts[1], parts[0])
+        first = (0, W, lv.x + W)[a]
+        start, count = ((lv.x - W, W), (0, lv.x), (0, W))[a]
+        for k in range(count):
+            x = first + k
+            strip = jnp.where(edge, pltpu.roll(both, (256 - 8 * (start + k) - W) % 128, 1), 0.0)
             if lv.z == 64:
-                plane = jnp.where(lane >= 64, pltpu.roll(plane, 64, 1), plane)
-            packed = jnp.where(lane // 8 == k, pltpu.roll(plane, (8 * k + W) % 128, 1), packed)
-        pz[tile] = packed
-    finish = send_pair("gz", counts["gz"], ((pz, lz.at[0]), (pz, lz.at[1])), sends.at[2], recvs.at[2])
-    yield
-    finish()
-    edge = (lane < W) | (lane >= 128 - W)
-    for tile in range(lv.tiles):
-        both = jnp.where(lane % 8 >= W, lz[0, tile], lz[1, tile])
-        for k in range(min(16, lv.xe - 16 * tile)):
-            x = 16 * tile + k
-            strip = jnp.where(edge, pltpu.roll(both, (256 - 8 * k - W) % 128, 1), 0.0)
-            if lv.z == 64:
-                v[x] = jnp.where(lane < 64, v[x], jnp.where(lane >= 128 - W, strip, pltpu.roll(strip, 64, 1)))
+                v[x] = jnp.where(side < 64, v[x], jnp.where(side >= 128 - W, strip, pltpu.roll(strip, 64, 1)))
             else:
                 v[x, :, lv.z : lv.z + 128] = strip
     yield
 
 
 def gather(buf, sends, recvs, counts):
-    at = {axis: lax.axis_index(axis) for axis in counts}
-    prefix = {"gz": (at["gx"], at["gy"]), "gy": (at["gx"],), "gx": ()}
-    base = 0
-    for axis in ("gz", "gy", "gx"):
-        me, n = at[axis], counts[axis]
+    me = {axis: lax.axis_index(axis) for axis in counts}
+    nx, ny, nz = counts["gx"], counts["gy"], counts["gz"]
+
+    def run(steps, base):
         copies = []
-        for k in range(1, n):
-            block = buf.at[prefix[axis] + (me,)]
-            copy = pltpu.make_async_remote_copy(
-                block, block, sends.at[base + k - 1], recvs.at[base + k - 1],
-                device_id={axis: lax.rem(me + k, n)}, device_id_type=MESH)
+        for at, (target, mine, theirs) in enumerate(steps):
+            pair = (sends.at[base + at], recvs.at[base + at])
+            copy = pltpu.make_async_remote_copy(mine, mine, *pair, device_id=target, device_id_type=MESH)
             copy.start()
-            source = buf.at[prefix[axis] + (lax.rem(me + n - k, n),)]
-            arrive = pltpu.make_async_remote_copy(
-                source, source, sends.at[base + k - 1], recvs.at[base + k - 1],
-                device_id={axis: lax.rem(me + k, n)}, device_id_type=MESH)
-            copies.append((copy, arrive))
+            copies.append((copy, pltpu.make_async_remote_copy(
+                theirs, theirs, *pair, device_id=target, device_id_type=MESH)))
         yield
         for copy, arrive in copies:
             copy.wait_send()
             arrive.wait_recv()
-        base += n - 1
-    yield
-
-
-def together(*steps):
-    for _ in zip(*steps):
-        pass
+
+    steps = []
+    for b in range(ny):
+        for c in range(nz):
+            if b or c:
+                target = {"gy": lax.rem(me["gy"] + b, ny), "gz": lax.rem(me["gz"] + c, nz)}
+                source = buf.at[me["gx"], lax.rem(me["gy"] + ny - b, ny), lax.rem(me["gz"] + nz - c, nz)]
+                steps.append((target, buf.at[me["gx"], me["gy"], me["gz"]], source))
+    yield from run(steps, 0)
+    base = len(steps)
+    steps = [({"gx": lax.rem(me["gx"] + a, nx)}, buf.at[me["gx"]], buf.at[lax.rem(me["gx"] + nx - a, nx)]) for a in range(1, nx)]
+    yield from run(steps, base)
+
+
+def drain(*steps):
+    steps = list(steps)
+    while steps:
+        steps = [step for step in steps if next(step, steps) is not steps]
+
+
+def batches(low, high, size, body):
+    whole = (high - low) // size
+    if whole:
+        def run(step, carry):
+            body(low + step * size, size)
+            return carry
+
+        lax.fori_loop(0, whole, run, 0)
+    if low + whole * size < high:
+        body(low + whole * size, high - low - whole * size)
 
 
 def prepare(lv, k, fx, fy, fz, dd, iv):
-    def body(x, carry):
-        kx = k[x]
-        below = 0.5 * (k[jnp.maximum(x - 1, 0)] + kx)
-        above = 0.5 * (kx + k[jnp.minimum(x + 1, lv.xe - 1)])
-        second = 0.5 * (up(kx, 0) + kx)
-        third = 0.5 * (up(kx, 1) + kx)
-        total = below + above + second + down(second, 0) + third + down(third, 1)
-        fx[x], fy[x], fz[x], dd[x] = below, second, third, total
-        iv[x] = jnp.where(kx > 0.0, 1.0 / total, 0.0)
-        return carry
-
-    lax.fori_loop(0, lv.xe, body, 0)
+    def body(first, count):
+        made = []
+        for x in [first + i for i in range(count)]:
+            kx = k[x]
+            below = 0.5 * (k[jnp.maximum(x - 1, 0)] + kx)
+            above = 0.5 * (kx + k[jnp.minimum(x + 1, lv.xe - 1)])
+            second = 0.5 * (up(kx, 0) + kx)
+            third = 0.5 * (up(kx, 1) + kx)
+            total = below + above + second + down(second, 0) + third + down(third, 1)
+            made.append((x, below, second, third, total, jnp.where(kx > 0.0, 1.0 / total, 0.0)))
+        for x, *values in made:
+            for ref, value in zip((fx, fy, fz, dd, iv), values):
+                ref[x] = value
+
+    batches(0, lv.xe, 4 if lv.ze == 128 else 2, body)
 
 
 def around(v, x, mid, faces):
@@ -173,47 +182,51 @@
     return summed + third * up(mid, 1) + down(third * mid, 1)
 
 
-def half_sweep(lv, v, g, faces, iv, colour, batch):
+def half_sweep(lv, v, g, faces, iv, colour, reach):
     parity = iota((lv.ye, lv.ze), 0) + iota((lv.ye, lv.ze), 1)
 
-    def body(step, carry):
+    def body(first, count):
         fresh = []
-        for k in range(batch):
-            x = 1 + step * batch + k
+        for x in [first + i for i in range(count)]:
             mid = v[x]
             value = (g[x] + around(v, x, mid, faces)) * iv[x]
-            fresh.append((x, jnp.where((parity + x) % 2 == colour, value, mid)))
+            fresh.append((x, jnp.where(((parity + x) & 1) == colour, value, mid)))
         for x, value in fresh:
             v[x] = value
-        return carry
-
-    lax.fori_loop(0, (lv.xe - 2) // batch, body, 0)
+
+    batches(W - reach, W + lv.x + reach, 10 if lv.ze == 128 else 6, body)
 
 
 def residual_pairs(lv, v, g, faces, dd, pairs):
-    def body(i, carry):
-        total = jnp.zeros((lv.ye, lv.ze), F32)
-        for k in range(2):
-            x = W + 2 * i + k
-            mid = v[x]
-            total = total + (g[x] - dd[x] * mid + around(v, x, mid, faces))
-        pairs[i] = total[0 : lv.y, 0 : lv.own]
-        return carry
-
-    lax.fori_loop(0, lv.x // 2, body, 0)
+    def body(first, count):
+        made = []
+        for i in [first + j for j in range(count)]:
+            total = jnp.zeros((lv.ye, lv.ze), F32)
+            for k in range(2):
+                x = W + 2 * i + k
+                mid = v[x]
+                total = total + (g[x] - dd[x] * mid + around(v, x, mid, faces))
+            made.append((i, total))
+        for i, total in made:
+            pairs[i] = total[0 : lv.y, 0:128]
+
+    batches(0, lv.x // 2, 4, body)
 
 
 def open_halo(lv, p, v, g, dd):
     parity = iota((lv.ye, lv.ze), 0) + iota((lv.ye, lv.ze), 1)
 
-    def body(x, carry):
-        red = (parity + x) % 2 == 0
-        px = p[x]
-        v[x] = jnp.where(red, px, 0.0)
-        g[x] = jnp.where(red, px * dd[x], px)
-        return carry
-
-    lax.fori_loop(0, lv.xe, body, 0)
+    def body(first, count):
+        made = []
+        for x in [first + i for i in range(count)]:
+            red = ((parity + x) & 1) == 0
+            px = p[x]
+            made.append((x, jnp.where(red, px, 0.0), jnp.where(red, px * dd[x], px)))
+        for x, value, source in made:
+            v[x] = value
+            g[x] = source
+
+    batches(0, lv.xe, 4, body)
 
 
 def fold_rows(pairs, rows):
@@ -368,10 +381,22 @@
         r[name][...] = jnp.zeros(r[name].shape, F32)
 
     barrier = pltpu.get_barrier_semaphore()
-    for axis, n in counts.items():
-        for k in range(1, n):
-            pl.semaphore_signal(
-                barrier, inc=1, device_id={axis: lax.rem(at[axis] + k, n)}, device_id_type=MESH)
+    expected = 0
+    for offset in NEAR:
+        target, exists = near(offset, counts)
+
+        @pl.when(exists)
+        def _():
+            pl.semaphore_signal(barrier, inc=1, device_id=target, device_id_type=MESH)
+
+        expected = expected + jnp.where(exists, 1, 0)
+    others = [{"gx": lax.rem(at["gx"] + k, counts["gx"])} for k in range(1, counts["gx"])]
+    for b in range(counts["gy"]):
+        for c in range(groups):
+            if b or c:
+                others.append({"gy": lax.rem(at["gy"] + b, counts["gy"]), "gz": lax.rem(at["gz"] + c, groups)})
+    for target in others:
+        pl.semaphore_signal(barrier, inc=1, device_id=target, device_id_type=MESH)
 
     pack_boxes(slots, ids, r["outgoing"], boxes, groups)
     K0, K1 = r["K0"], r["K1"]
@@ -383,7 +408,7 @@
         r["pairsm"][i] = K1[W + 2 * i, 0 : mid.y, :] + K1[W + 2 * i + 1, 0 : mid.y, :]
     here = (at["gx"], at["gy"], at["gz"])
     coarse_low(r["pairsm"], mid.x // 2, mid.y, mid.z // 2, r["tmp"], r["gk"].at[here])
-    pl.semaphore_wait(barrier, sum(counts.values()) - len(counts))
+    pl.semaphore_wait(barrier, expected + len(others))
 
     moves = []
     me = at["gz"]
@@ -402,10 +427,9 @@
     def bufs(n, tail):
         return tuple(r[b + tail].at[n] for b in ("py", "ly", "pz", "lz", "es", "er"))
 
-    steps = [
-        exchange(fine, K0, bufs(0, ""), counts), exchange(mid, K1, bufs(0, "m"), counts),
-        gather(r["gk"], r["gs"].at[0], r["gr"].at[0], counts)]
-    for step in steps:
+    fine_halo, mid_halo = exchange(fine, K0, bufs(0, ""), counts), exchange(mid, K1, bufs(0, "m"), counts)
+    low_gather = gather(r["gk"], r["gs"].at[0], r["gr"].at[0], counts)
+    for step in (fine_halo, mid_halo, low_gather):
         next(step)
     lane = iota((BOX * BOX, 128), 1)
     folded = iota((BOX * BOX, 128), 0) % BOX == lane % BOX
@@ -417,7 +441,7 @@
         arrive.wait_recv()
     source = place_boxes(r["incoming"], owner, r["lhs"], r["rhs"], boxes, groups)
     source = source.reshape(fine.x, fine.y, 128)
-    together(*steps)
+    drain(fine_halo)
 
     faces0 = (r["fx0"], r["fy0"], r["fz0"])
     faces1 = (r["fx1"], r["fy1"], r["fz1"])
@@ -430,11 +454,13 @@
         r["P0"][W + x, 0 : fine.y, 0:128] = jnp.where(red, source[x] * iv0[W + x, 0 : fine.y, 0:128], source[x])
     step = exchange(fine, r["P0"], bufs(1, ""), counts)
     next(step)
+    drain(mid_halo)
     prepare(mid, K1, *faces1, dd1, iv1)
-    together(step)
+    next(low_gather)
+    drain(step)
     open_halo(fine, r["P0"], v0, g0, dd0)
-    for colour in (1, 0, 1):
-        half_sweep(fine, v0, g0, faces0, iv0, colour, 2)
+    for reach, colour in ((3, 1), (2, 0), (1, 1)):
+        half_sweep(fine, v0, g0, faces0, iv0, colour, reach)
     residual_pairs(fine, v0, g0, faces0, dd0, r["pairs"])
 
     source1 = coarse_mid(r["pairs"], fine.x, fine.y)
@@ -445,17 +471,18 @@
         r["P1"][W + x, 0 : mid.y, :] = jnp.where(red, scaled * iv1[W + x, 0 : mid.y, :], scaled)
     step = exchange(mid, r["P1"], bufs(1, "m"), counts)
     next(step)
+    drain(low_gather)
     spread_low(r["gk"], r["k2"], counts, 1)
-    together(step)
+    drain(step)
     open_halo(mid, r["P1"], v1, g1, dd1)
-    for colour in (1, 0, 1):
-        half_sweep(mid, v1, g1, faces1, iv1, colour, 2)
+    for reach, colour in ((3, 1), (2, 0), (1, 1)):
+        half_sweep(mid, v1, g1, faces1, iv1, colour, reach)
     residual_pairs(mid, v1, g1, faces1, dd1, r["pairsm"])
     for i in range(mid.x // 2):
         r["pairsm"][i] = r["pairsm"][i] * 0.25
     coarse_low(r["pairsm"], mid.x // 2, mid.y, mid.z // 2, r["tmp"], r["gf"].at[here])
     r["E1"][W : W + mid.x, 0 : mid.y, :] = v1[W : W + mid.x, 0 : mid.y, :]
-    together(
+    drain(
         gather(r["gf"], r["gs"].at[1], r["gr"].at[1], counts),
         exchange(mid, r["E1"], bufs(2, "m"), counts))
 
@@ -482,8 +509,8 @@
         for k in range(2):
             x = 2 * q + k
             E1[x] = jnp.where(K1[x] > 0.0, E1[x] + r["wide"][...], 0.0)
-    for colour in (0, 1, 0, 1):
-        half_sweep(mid, E1, g1, faces1, iv1, colour, 2)
+    for reach, colour in ((3, 0), (2, 1), (1, 0), (0, 1)):
+        half_sweep(mid, E1, g1, faces1, iv1, colour, reach)
 
     matrix = jnp.where(iota((128, 128), 0) == iota((128, 128), 1) // 2, 1.0, 0.0).astype(F32)
     fresh = dot(E1[W : W + mid.x, 0 : mid.y, :].reshape(mid.x * mid.y, 128), matrix).reshape(mid.x, mid.y, 128)
@@ -494,9 +521,9 @@
         for k in range(2):
             x = W + 2 * i + k
             Q0[x, 0 : fine.y, 0:128] = v0[x, 0 : fine.y, 0:128] + r["wide"][...]
-    together(exchange(fine, Q0, bufs(2, ""), counts))
-    for colour in (0, 1, 0, 1):
-        half_sweep(fine, Q0, g0, faces0, iv0, colour, 2)
+    drain(exchange(fine, Q0, bufs(2, ""), counts))
+    for reach, colour in ((3, 0), (2, 1), (1, 0), (0, 1)):
+        half_sweep(fine, Q0, g0, faces0, iv0, colour, reach)
     out[...] = Q0[W : W + fine.x, 0 : fine.y, 0:128]
 
 
@@ -506,19 +533,19 @@
     planes, rows, lanes = 4 * counts["gx"], 4 * counts["gy"], 32 * counts["gz"]
     groups, boxes = counts["gz"], z // BOX
     cells = old_slots.shape[3]
-    partners = sum(counts.values()) - len(counts)
+    partners = counts["gx"] - 1 + counts["gy"] * groups - 1
     vmem = lambda *shape: pltpu.VMEM(shape, F32)
     dma = lambda *shape: pltpu.SemaphoreType.DMA(shape)
     scratch = {}
     for level, tail, names in ((fine, "", ("K0", "P0", "Q0")), (mid, "m", ("K1", "P1", "E1"))):
         for name in names:
             scratch[name] = vmem(*level.shape)
-        scratch["py" + tail] = vmem(3, 2, level.xe, W, 128)
+        scratch["py" + tail] = vmem(3, 2, level.x, W, 128)
         scratch["ly" + tail] = vmem(3, 2, level.xe, W, 128)
-        scratch["pz" + tail] = vmem(3, level.tiles, level.ye, 128)
-        scratch["lz" + tail] = vmem(3, 2, level.tiles, level.ye, 128)
-        scratch["es" + tail] = dma(3, 3, 2)
-        scratch["er" + tail] = dma(3, 3, 2)
+        scratch["pz" + tail] = vmem(3, level.y, 128)
+        scratch["lz" + tail] = vmem(3, 2, 3, 3, level.y, 128)
+        scratch["es" + tail] = dma(3, len(NEAR))
+        scratch["er" + tail] = dma(3, len(NEAR))
         scratch["pairs" + tail] = vmem(level.x // 2, level.y, 128)
     for level, tail in ((fine, "0"), (mid, "1")):
         for name in ("fx", "fy", "fz", "dd", "iv", "v", "g"):

time: 77.5 us -> 49.7 us (0.64)
  Pallas kernels: 75.8 us -> 47.8 us
    pallas_call x1, Pallas kernels: 75.8 us -> 47.8 us  [per_device(): pl.pallas_call(functools.partial(kernel, fine, mid, counts, tuple(scratch...]
where the time goes in v2:
time: 49.7 us; the launch traced here: 49.3 us
  Pallas kernels  47.8 us (96%)
  local copies, waits for them, and re-layouts  1.57 us (3%)
    pallas_call x1, Pallas kernels, per_device(): pl.pallas_call(functools.partial(kernel, fine, mid, counts, tuple(scratch...  47.8 us
    unnamed x1, local copies, waits for them, and re-layouts  1.57 us

profile of v2, /device:TPU:1, one launch (start us, length us, event | category | flops | bytes accessed | tf_op | source)
XLA Modules:
  0.0 49.3 jit_solution(7582736062175290072)
XLA Ops:
  0.0 47.8 %shard_map.46 = f32[16,16,128]{2,1,0:T(8,128)} custom-call(bf16[1,1,8,4096]{3,2,1,0:T(8,128)(2,1)} %slots.1, s32[1,1,8]{2,1,0:T(1,128)} %ids.1, s32[1,1,32]{2,1,0:T(1,128)} %owner.1, f32[16,16,128]{2,1,0:T(8,128)} %coef.1), custom_call_target="tpu_custom_call" | custom-call | tf_op jit(solution)/shard_map/pallas_call | solution.py:562
  47.8 1.6 %copy.6 = f32[16,16,128]{2,1,0:T(8,128)} copy(f32[16,16,128]{2,1,0:T(8,128)} %shard_map.46) | data formatting | bytes 262144
